TPU v7x, 32 devices: a whole 2x2x4 slice. The times are simulated.
32 devices in a mesh: dp: 4 (over y, x), tensor: 8 (over z, core).
Axes of the slice: x: 2, y: 2, z: 4, core: 2. Of those that a mesh axis runs over, the one named last changes fastest.
Arguments:
- attention_output: bfloat16 [512, 8192], P('dp', 'tensor'), may hold values from -6 to 6
- residual: bfloat16 [512, 8192], P('dp', 'tensor'), may hold values from -6 to 6
- output_weight: bfloat16 [8192, 8192], P('tensor'), may hold values from -0.09375 to 0.09375
- down_factors: bfloat16 [256, 8192, 16], P('dp', 'tensor'), may hold values from -0.0625 to 0.0625
- up_factors: bfloat16 [256, 16, 8192], P('dp', None, 'tensor'), may hold values from -1.5 to 1.5
- adapter_index: int32 [512], P('dp'), may hold values from 0 to 255, as said below
Outputs:
- layer_out: bfloat16 [512, 8192], P('dp', 'tensor')
Inputs may be any that keep to these rules, and one draw needn't show every extreme that they name: adapter_index // 64 is the request group that owns the adapter. Of one group's 128 rows at most 64 use adapters owned by one group, and in every draw some group owns the adapters of exactly 64 rows of every group.
All inputs are finite; a program needn't handle non-finite values.
Results may differ from a plain program's by a relative error of at most 0.0041.
Values may be sent and summed in bfloat16 or wider, within the bound.
A program may use at most 64 MiB of HBM per device.

v0:
```python
import functools

import jax
import jax.numpy as jnp
from jax import lax
from jax.experimental import pallas as pl
from jax.experimental.pallas import tpu as pltpu
from jax.sharding import PartitionSpec as P

MESH = pl.DeviceIdType.MESH
F32 = jnp.float32
BF16 = jnp.bfloat16
LANES = 128
PIECES = 2
AHEAD = 3


def kernel(
    groups, members, rank, owned, halves,
    x_ref, res_ref, idx_ref, w_ref, down_ref, up_ref, out_ref,
    wbuf, dbuf, ubuf, rbuf, own, psend, precv, rrecv, lrecv, rsend, lsend,
    xsend, xrecv, terms, packed, arp, arz, esend, eback,
    w_sem, d_sem, ps_sem, pr_sem, rs_sem, rr_sem, ls_sem, lr_sem,
    xs_sem, xr_sem, as_sem, ar_sem, zs_sem, zr_sem, es_sem, er_sem,
):
    chips = members // 2
    g = lax.axis_index("dp")
    t = lax.axis_index("tensor")
    z = t // 2
    c = lax.rem(t, 2)
    partner = z * 2 + (1 - c)
    rows, depth = x_ref.shape
    width = out_ref.shape[1]
    part = xrecv.shape[2]
    cap = part * halves
    slots = groups * part
    low = z < chips // 2
    piece = width // PIECES

    def block_chip(i):
        return jnp.where(low, chips - 1 - i, i)

    def weight_copy(n):
        column = block_chip(n // 2) * 2 + (1 - c if n % 2 == 0 else c)
        start = pl.multiple_of(column * width, LANES)
        return pltpu.make_async_copy(
            w_ref.at[:, pl.ds(start, width)], wbuf.at[n], w_sem.at[n]
        )

    down_copy = pltpu.make_async_copy(down_ref, dbuf, d_sem.at[0])
    up_copy = pltpu.make_async_copy(up_ref, ubuf, d_sem.at[1])
    res_copy = pltpu.make_async_copy(res_ref, rbuf, d_sem.at[2])
    for n in range(min(AHEAD, members)):
        weight_copy(n).start()

    barrier = pltpu.get_barrier_semaphore()
    pl.semaphore_signal(barrier, inc=1, device_id=(g, partner), device_id_type=MESH)
    for k in range(1, chips):
        peer = lax.rem(z + k, chips) * 2 + c
        pl.semaphore_signal(barrier, inc=1, device_id=(g, peer), device_id_type=MESH)
    for k in range(1, groups):
        pl.semaphore_signal(
            barrier, inc=1, device_id=(lax.rem(g + k, groups), t), device_id_type=MESH
        )

    idx_row = idx_ref[...]
    r_i = lax.broadcasted_iota(jnp.int32, (rows, rows), 0)
    c_i = lax.broadcasted_iota(jnp.int32, (rows, rows), 1)
    idx_full = jnp.broadcast_to(idx_row, (rows, rows))
    idx_col = jnp.sum(jnp.where(r_i == c_i, idx_full, 0), axis=1, keepdims=True)
    own_row = idx_row // owned
    own_col = idx_col // owned
    same = own_col == own_row
    rank_row = jnp.sum(jnp.where(same & (r_i < c_i), 1, 0), axis=0, keepdims=True)
    rank_col = jnp.sum(jnp.where(same & (c_i < r_i), 1, 0), axis=1, keepdims=True)

    def slot_of(place_rank, owner, h):
        inside = place_rank - h * part
        keep = (inside >= 0) & (inside < part)
        return jnp.where(keep, owner * part + inside, -1)

    number_row = lax.rem(idx_row, owned) + 1
    step = min(256, depth)

    def row_copy(h, k):
        to = lax.rem(g + k, groups)
        return pltpu.make_async_remote_copy(
            src_ref=xsend.at[h, to], dst_ref=xrecv.at[h, g],
            send_sem=xs_sem.at[h * groups + k], recv_sem=xr_sem.at[h * groups + g],
            device_id=(to, t), device_id_type=MESH,
        )

    def row_wait(h, k):
        source = lax.rem(g + k, groups)
        pltpu.make_async_remote_copy(
            src_ref=xsend.at[h, source], dst_ref=xrecv.at[h, source],
            send_sem=xs_sem.at[h * groups + k], recv_sem=xr_sem.at[h * groups + source],
            device_id=(source, t), device_id_type=MESH,
        ).wait_recv()

    for h in range(halves):
        slot_row = slot_of(rank_row, own_row, h)
        placing = lax.broadcasted_iota(jnp.int32, (slots, rows), 0) == slot_row
        request = jnp.sum(jnp.where(placing, number_row, 0), axis=1, keepdims=True)
        place = jnp.where(placing, 1.0, 0.0).astype(BF16)
        numbers = jnp.broadcast_to(request.astype(F32), (slots, LANES)).astype(BF16)
        for k in range(groups):
            xsend[h, k, :, depth:] = numbers[k * part:(k + 1) * part]
        for j in range(depth // step):
            moved = jnp.dot(
                place, x_ref[:, j * step:(j + 1) * step], preferred_element_type=F32
            ).astype(BF16)
            for k in range(groups):
                xsend[h, k, :, j * step:(j + 1) * step] = moved[k * part:(k + 1) * part]
        if h == 0:
            pl.semaphore_wait(barrier, chips + groups - 1)
        for k in range(1, groups):
            row_copy(h, k).start()
        xrecv[h, g] = xsend[h, g]
        if h == 0:
            down_copy.start()

    tile = min(256, piece)
    tiles = piece // tile

    def pair_copy(chip, q):
        k = chip * PIECES + q
        return pltpu.make_async_remote_copy(
            src_ref=psend.at[k], dst_ref=precv.at[k], send_sem=ps_sem.at[k],
            recv_sem=pr_sem.at[k], device_id=(g, partner), device_id_type=MESH,
        )

    strip = 16

    def hop(chip, q, to, send, recv, s_sem, r_sem):
        k = chip * PIECES + q
        return pltpu.make_async_remote_copy(
            src_ref=send.at[k], dst_ref=recv.at[k], send_sem=s_sem.at[k],
            recv_sem=r_sem.at[k], device_id=(g, to * 2 + c), device_id_type=MESH,
        )

    right = functools.partial(hop, send=rsend, recv=rrecv, s_sem=rs_sem, r_sem=rr_sem)
    left = functools.partial(hop, send=lsend, recv=lrecv, s_sem=ls_sem, r_sem=lr_sem)

    def pass_on(chip, q, first, to, make, send, recv):
        k = chip * PIECES + q

        @pl.when(first)
        def _():
            @pl.loop(0, rows // strip)
            def _(n):
                at = pl.ds(pl.multiple_of(n * strip, strip), strip)
                send[k, at] = (own[k, at] + precv[k, at].astype(F32)).astype(BF16)

        @pl.when(jnp.logical_not(first))
        def _():
            make(chip, q, to).wait_recv()

            @pl.loop(0, rows // strip)
            def _(n):
                at = pl.ds(pl.multiple_of(n * strip, strip), strip)
                send[k, at] = (
                    own[k, at] + precv[k, at].astype(F32) + recv[k, at].astype(F32)
                ).astype(BF16)

        make(chip, q, to).start()

    def chain(turn, q):
        @pl.when(z <= turn)
        def _():
            pass_on(chips - 1 - turn + z, q, z == 0, z + 1, right, rsend, rrecv)

        @pl.when(chips - 1 - z <= turn)
        def _():
            pass_on(turn - chips + 1 + z, q, z == chips - 1, z - 1, left, lsend, lrecv)

    def start_weights(n):
        if n + AHEAD < members:
            weight_copy(n + AHEAD).start()

    def project(i):
        chip = block_chip(i)
        weight_copy(2 * i).wait()
        start_weights(2 * i)
        for q in range(PIECES):
            for n in range(tiles):
                psend[chip * PIECES + q, :, n * tile:(n + 1) * tile] = jnp.dot(
                    x_ref[...],
                    wbuf[2 * i, :, q * piece + n * tile:q * piece + (n + 1) * tile],
                    preferred_element_type=F32,
                ).astype(BF16)
            pair_copy(chip, q).start()
        weight_copy(2 * i + 1).wait()
        start_weights(2 * i + 1)
        for q in range(PIECES):
            for n in range(tiles):
                own[chip * PIECES + q, :, n * tile:(n + 1) * tile] = jnp.dot(
                    x_ref[...],
                    wbuf[2 * i + 1, :, q * piece + n * tile:q * piece + (n + 1) * tile],
                    preferred_element_type=F32,
                )
            if i == 0:
                pair_copy(chip, q).wait_recv()
                if chips > 1:
                    chain(0, q)

    def paired(i):
        for q in range(PIECES):
            pair_copy(block_chip(i), q).wait_recv()

    lane_group = lax.broadcasted_iota(jnp.int32, (slots, LANES), 1) // rank
    lane_number = (lane_group + 1).astype(F32)
    per_tile = LANES // rank
    tile_count = owned * rank // LANES
    pair = 2 if tile_count % 2 == 0 else 1
    pack_rows = slots // per_tile
    pack_group = lax.broadcasted_iota(jnp.int32, (pack_rows, LANES), 1) // rank

    def spread_lanes(v):
        shift = rank
        while shift < LANES:
            v = v + pltpu.roll(v, shift, 1)
            shift *= 2
        return v

    def term_pair(h):
        return pltpu.make_async_remote_copy(
            src_ref=packed.at[h], dst_ref=arp.at[h], send_sem=as_sem.at[h],
            recv_sem=ar_sem.at[h], device_id=(g, partner), device_id_type=MESH,
        )

    def term_copy(h, k):
        to = lax.rem(z + k, chips)
        return pltpu.make_async_remote_copy(
            src_ref=arz.at[h, z], dst_ref=arz.at[h, z], send_sem=zs_sem.at[h * chips + k],
            recv_sem=zr_sem.at[h * chips + z], device_id=(g, to * 2 + c), device_id_type=MESH,
        )

    def term_wait(h, k):
        source = lax.rem(z + k, chips)
        pltpu.make_async_remote_copy(
            src_ref=arz.at[h, source], dst_ref=arz.at[h, source],
            send_sem=zs_sem.at[h * chips + k], recv_sem=zr_sem.at[h * chips + source],
            device_id=(g, source * 2 + c), device_id_type=MESH,
        ).wait_recv()

    def wanted_of(h):
        return xrecv[h, :, :, depth:].reshape(slots, LANES).astype(F32)

    def shrink_rows(h):
        for k in range(1, groups):
            row_wait(h, k)
        if h == 0:
            down_copy.wait()
            up_copy.start()
            res_copy.start()
        wanted = wanted_of(h)
        flat = xrecv[h, :, :, :depth].reshape(slots, depth)
        terms[...] = jnp.zeros_like(terms)

        @pl.loop(0, tile_count // pair)
        def _(m):
            at = pl.ds(pl.multiple_of(m * pair * LANES, LANES), pair * LANES)
            every = lax.dot_general(
                flat, dbuf[at, :], (((1,), (1,)), ((), ())), preferred_element_type=F32
            )
            for p in range(pair):
                first_number = ((m * pair + p) * per_tile).astype(F32)
                terms[...] += jnp.where(
                    wanted == lane_number + first_number, every[:, p * LANES:(p + 1) * LANES], 0.0
                )

        chosen_terms = spread_lanes(terms[...])
        mine = jnp.zeros((pack_rows, LANES), F32)
        for p in range(per_tile):
            mine = jnp.where(
                pack_group == p, chosen_terms[p * pack_rows:(p + 1) * pack_rows], mine
            )
        packed[h] = mine
        term_pair(h).start()

    def sum_send(h):
        term_pair(h).wait_recv()
        arz[h, z] = packed[h] + arp[h]
        for k in range(1, chips):
            term_copy(h, k).start()

    def back_copy(h, k):
        to = lax.rem(g + k, groups)
        return pltpu.make_async_remote_copy(
            src_ref=esend.at[h, to], dst_ref=eback.at[h, g],
            send_sem=es_sem.at[h * groups + k], recv_sem=er_sem.at[h * groups + g],
            device_id=(to, t), device_id_type=MESH,
        )

    def back_wait(h, k):
        source = lax.rem(g + k, groups)
        pltpu.make_async_remote_copy(
            src_ref=esend.at[h, source], dst_ref=eback.at[h, source],
            send_sem=es_sem.at[h * groups + k], recv_sem=er_sem.at[h * groups + source],
            device_id=(source, t), device_id_type=MESH,
        ).wait_recv()

    wide = min(256, width)

    def expand_rows(h):
        for k in range(1, chips):
            term_wait(h, k)
        total = arz[h, 0]
        for k in range(1, chips):
            total = total + arz[h, k]
        total = total.astype(BF16).astype(F32)
        if h == 0:
            up_copy.wait()
        wanted = wanted_of(h)
        shrink = jnp.concatenate(
            [spread_lanes(jnp.where(pack_group == p, total, 0.0)) for p in range(per_tile)],
            axis=0,
        )
        spread = jnp.concatenate(
            [
                jnp.where(wanted == lane_number + float(m * per_tile), shrink, 0.0).astype(BF16)
                for m in range(tile_count)
            ],
            axis=1,
        )

        @pl.loop(0, width // wide)
        def _(n):
            cols = pl.ds(pl.multiple_of(n * wide, LANES), wide)
            grown = jnp.dot(spread, ubuf[:, cols], preferred_element_type=F32).astype(BF16)
            for k in range(groups):
                esend[h, k, :, cols] = grown[k * part:(k + 1) * part]

        for k in range(1, groups):
            back_copy(h, k).start()
        eback[h, g] = esend[h, g]

    last = halves - 1
    early = chips // 2
    project(0)
    if chips > 1:
        project(1)
    shrink_rows(0)
    for i in range(2, chips):
        project(i)
        paired(i - 1)
        if i == 2:
            sum_send(0)
        if i - 1 < early and i - 1 < chips - 1:
            chain(i - 1, 0)
        if i == 2 and halves > 1:
            shrink_rows(1)
        if i - 1 < early and i - 1 < chips - 1:
            for q in range(1, PIECES):
                chain(i - 1, q)
    if chips > 1:
        paired(chips - 1)
    if chips < 3:
        sum_send(0)
        if halves > 1:
            shrink_rows(1)
    if halves > 1:
        sum_send(1)
    expand_rows(0)
    for turn in range(early, chips - 1):
        chain(turn, 0)
    if halves > 1:
        expand_rows(1)
    for turn in range(early, chips - 1):
        for q in range(1, PIECES):
            chain(turn, q)

    res_copy.wait()

    def branch_of(h, q, n):
        slot_col = slot_of(rank_col, own_col, h)
        unplace = jnp.where(
            lax.broadcasted_iota(jnp.int32, (rows, slots), 1) == slot_col, 1.0, 0.0
        ).astype(BF16)
        first = q * piece + n * tile
        back = eback[h, :, :, first:first + tile].reshape(slots, tile)
        return jnp.dot(unplace, back, preferred_element_type=F32)

    for h in range(halves):
        for k in range(1, groups):
            back_wait(h, k)
        for q in range(PIECES):
            for n in range(tiles):
                cols = slice(n * tile, (n + 1) * tile)
                first = q * piece + n * tile
                value = own[z * PIECES + q, :, cols] + branch_of(h, q, n)
                if h == 0:
                    value = (
                        value + precv[z * PIECES + q, :, cols].astype(F32)
                        + rbuf[:, first:first + tile].astype(F32)
                    )
                own[z * PIECES + q, :, cols] = value

    for q in range(PIECES):
        mine_at = z * PIECES + q

        def finish(use_right, use_left):
            @pl.loop(0, rows // strip)
            def _(n):
                at = pl.ds(pl.multiple_of(n * strip, strip), strip)
                value = own[mine_at, at]
                if use_right:
                    value = value + rrecv[mine_at, at].astype(F32)
                if use_left:
                    value = value + lrecv[mine_at, at].astype(F32)
                out_ref[at, q * piece:(q + 1) * piece] = value.astype(BF16)

        if chips == 1:
            finish(False, False)
        else:
            @pl.when(z == 0)
            def _():
                left(z, q, z).wait_recv()
                finish(False, True)

            @pl.when(z == chips - 1)
            def _():
                right(z, q, z).wait_recv()
                finish(True, False)

            @pl.when((z > 0) & (z < chips - 1))
            def _():
                right(z, q, z).wait_recv()
                left(z, q, z).wait_recv()
                finish(True, True)

    for i in range(chips):
        for q in range(PIECES):
            pair_copy(i, q).wait_send()
    for h in range(halves):
        for k in range(1, groups):
            row_copy(h, k).wait_send()
            back_copy(h, k).wait_send()
        term_pair(h).wait_send()
        for k in range(1, chips):
            term_copy(h, k).wait_send()
    for chip in range(chips):
        for q in range(PIECES):
            @pl.when(z < chip)
            def _():
                right(chip, q, z + 1).wait_send()

            @pl.when(z > chip)
            def _():
                left(chip, q, z - 1).wait_send()


def body(attention_output, residual, output_weight, down_factors, up_factors, adapter_index):
    groups = lax.axis_size("dp")
    members = lax.axis_size("tensor")
    rows, depth = attention_output.shape
    owned, _, rank = down_factors.shape
    width = output_weight.shape[1] // members
    cap = 2 * rows // groups
    chips = members // 2
    halves = 2 if cap % 32 == 0 else 1
    part = cap // halves
    slots = groups * part
    pack = slots * rank // LANES
    piece = width // PIECES
    down = jnp.swapaxes(down_factors, 1, 2).reshape(owned * rank, depth)
    up = up_factors.reshape(owned * rank, width)
    vmem = pl.BlockSpec(memory_space=pltpu.VMEM)
    hbm = pl.BlockSpec(memory_space=pl.ANY)
    dma = pltpu.SemaphoreType.DMA
    hops = chips * PIECES
    return pl.pallas_call(
        functools.partial(kernel, groups, members, rank, owned, halves),
        out_shape=jax.ShapeDtypeStruct((rows, width), BF16),
        in_specs=[vmem, hbm, vmem, hbm, hbm, hbm],
        out_specs=vmem,
        scratch_shapes=[
            pltpu.VMEM((members, depth, width), BF16),
            pltpu.VMEM((owned * rank, depth), BF16),
            pltpu.VMEM((owned * rank, width), BF16),
            pltpu.VMEM((rows, width), BF16),
            pltpu.VMEM((hops, rows, piece), F32),
            pltpu.VMEM((hops, rows, piece), BF16),
            pltpu.VMEM((hops, rows, piece), BF16),
            pltpu.VMEM((hops, rows, piece), BF16),
            pltpu.VMEM((hops, rows, piece), BF16),
            pltpu.VMEM((hops, rows, piece), BF16),
            pltpu.VMEM((hops, rows, piece), BF16),
            pltpu.VMEM((halves, groups, part, depth + LANES), BF16),
            pltpu.VMEM((halves, groups, part, depth + LANES), BF16),
            pltpu.VMEM((slots, LANES), F32),
            pltpu.VMEM((halves, pack, LANES), F32),
            pltpu.VMEM((halves, pack, LANES), F32),
            pltpu.VMEM((halves, chips, pack, LANES), F32),
            pltpu.VMEM((halves, groups, part, width), BF16),
            pltpu.VMEM((halves, groups, part, width), BF16),
            dma((members,)), dma((3,)),
            dma((hops,)), dma((hops,)),
            dma((hops,)), dma((hops,)), dma((hops,)), dma((hops,)),
            dma((halves * groups,)), dma((halves * groups,)),
            dma((halves,)), dma((halves,)),
            dma((halves * chips,)), dma((halves * chips,)),
            dma((halves * groups,)), dma((halves * groups,)),
        ],
        compiler_params=pltpu.CompilerParams(
            collective_id=0, has_side_effects=True, vmem_limit_bytes=60 * 1024 * 1024
        ),
    )(attention_output, residual, adapter_index.reshape(1, rows), output_weight, down, up)


def solution(mesh):
    return jax.shard_map(
        body,
        mesh=mesh,
        in_specs=(
            P("dp", "tensor"),
            P("dp", "tensor"),
            P("tensor", None),
            P("dp", "tensor", None),
            P("dp", None, "tensor"),
            P("dp"),
        ),
        out_specs=P("dp", "tensor"),
        check_vma=False,
    )
```

profile of v0, /device:TPU:0, one launch (start us, length us, event | category | flops | bytes accessed | tf_op | source)
XLA Modules:
  0.0 33.9 jit_solution(17365075129733881543)
XLA Ops:
  0.0 32.2 %shard_map.64 = bf16[128,1024]{1,0:T(8,128)(2,1)} custom-call(bf16[128,1024]{1,0:T(8,128)(2,1)} %x_ref.1, bf16[128,1024]{1,0:T(8,128)(2,1)} %res_ref.1, s32[1,128]{1,0:T(1,128)} %bitcast.7, bf16[1024,8192]{1,0:T(8,128)(2,1)} %w_ref.1, bf16[1024,1024]{1,0:T(8,128)(2,1)} %bitcast.5, bf16[1024,1024]{1,0:T(8,128)(2,1)} %bitcast.6), custom_call_target="tpu_custom_call" | custom-call | tf_op jit(solution)/shard_map/pallas_call | solution.py:473
  32.2 1.7 %copy.8 = bf16[128,1024]{1,0:T(8,128)(2,1)} copy(bf16[128,1024]{1,0:T(8,128)(2,1)} %shard_map.64) | data formatting | bytes 524288
where the time goes:
time: 34.1 us; the launch traced here: 33.9 us
  Pallas kernels  32.2 us (94%)
  local copies, waits for them, and re-layouts  1.67 us (5%)
    pallas_call x1, Pallas kernels, body(): pl.pallas_call(functools.partial(kernel, groups, members, rank, owned, ha...  32.2 us
    unnamed x1, local copies, waits for them, and re-layouts  1.67 us

commit v1 on v0

v1 whole, which is shorter than its diff:
```python
import contextlib
import functools

import jax
import jax.numpy as jnp
from jax import lax
from jax.experimental import pallas as pl
from jax.experimental.pallas import tpu as pltpu
from jax.sharding import PartitionSpec as P

MESH = pl.DeviceIdType.MESH
F32 = jnp.float32
BF16 = jnp.bfloat16
LANES = 128
PIECES = 4
AHEAD = 4
FIRST = 2
ORDER = (
    ("near", 0), ("project", 0, 1), ("project", 0, 2), ("settle", 0, 0), ("far", 0),
    ("project", 0, 3), ("settle", 0, 1), ("place", 1), ("near", 1), ("far", 1), ("factors",),
    ("project", 0, 4), ("settle", 0, 2), ("project", 0, 5), ("settle", 0, 3),
    ("project", 0, 6), ("settle", 0, 4), ("project", 0, 7), ("settle", 0, 5),
    ("project", 1, 0), ("settle", 0, 6), ("project", 1, 1), ("settle", 0, 7), ("greet",),
    ("project", 1, 2), ("on", 0, 1, 0), ("on", 0, 1, 1),
    ("shrink", 0), ("project", 1, 3), ("project", 1, 4), ("meet",), ("sum", 0),
    ("on", 0, 1, 2), ("on", 0, 1, 3),
    ("project", 1, 5), ("settle", 1, 0), ("settle", 1, 1),
    ("first", 1, 0, 0), ("first", 1, 0, 1), ("first", 1, 0, 2),
    ("project", 1, 6), ("project", 1, 7),
    ("shrink", 1), ("on", 0, 2, 0), ("on", 0, 2, 1), ("sum", 1),
    ("settle", 1, 2), ("settle", 1, 3), ("settle", 1, 4), ("settle", 1, 5),
    ("settle", 1, 6), ("settle", 1, 7),
    ("first", 1, 0, 3),
    ("first", 1, 1, 0), ("first", 1, 1, 1), ("first", 1, 1, 2), ("first", 1, 1, 3),
    ("first", 1, 2, 0), ("first", 1, 2, 1), ("first", 1, 2, 2), ("first", 1, 2, 3),
    ("on", 0, 2, 2), ("on", 0, 2, 3),
    ("expand", 0), ("on", 1, 1, 0), ("expand", 1),
    ("on", 1, 1, 1), ("on", 1, 1, 2), ("on", 1, 1, 3),
    ("on", 1, 2, 0), ("on", 1, 2, 1), ("on", 1, 2, 2), ("on", 1, 2, 3),
)
scope = contextlib.nullcontext


def kernel(
    groups, members, rank, owned, halves, pieces,
    x_hbm, res_ref, idx_hbm, w_ref, down_ref, up_ref, out_ref,
    x_ref, idx_ref, wbuf, dbuf, ubuf, rbuf, own, psend, precv, rrecv, lrecv, rsend, lsend,
    xsend, xrecv, packed, arp, arz, esend, eback,
    w_sem, d_sem, ps_sem, pr_sem, rs_sem, ls_sem, hr_sem,
    xs_sem, xr_sem, as_sem, ar_sem, zs_sem, zr_sem, es_sem, er_sem, dp_sem, z_sem,
):
    chips = members // 2
    g = lax.axis_index("dp")
    t = lax.axis_index("tensor")
    z = t // 2
    c = lax.rem(t, 2)
    partner = z * 2 + (1 - c)
    rows, depth = x_ref.shape
    width = out_ref.shape[1]
    part = xrecv.shape[2]
    slots = groups * part
    low = z < chips // 2
    piece = width // pieces
    last_chip = chips - 1

    def core_of(chip):
        return (g, chip * 2 + c)

    bits = groups.bit_length() - 1
    cube = groups == 1 << bits

    def peer(k):
        if not cube:
            return lax.rem(g + k, groups)
        to = g
        for b in range(bits):
            if k >> b & 1:
                to = to + (1 << b) * (1 - 2 * lax.rem(g // (1 << b), 2))
        return to

    def source_of(k):
        return peer(k) if cube else lax.rem(g + groups - k, groups)

    near = [1 << b for b in range(bits)] if cube else list(range(1, groups))
    far = [k for k in range(1, groups) if k not in near]
    rounds = bits - 1 if far else 0

    barrier = pltpu.get_barrier_semaphore()
    pl.semaphore_signal(barrier, inc=1, device_id=(g, partner), device_id_type=MESH)

    @pl.when(z > 0)
    def _():
        pl.semaphore_signal(barrier, inc=1, device_id=core_of(z - 1), device_id_type=MESH)

    @pl.when(z < last_chip)
    def _():
        pl.semaphore_signal(barrier, inc=1, device_id=core_of(z + 1), device_id_type=MESH)

    for k in near:
        pl.semaphore_signal(barrier, inc=1, device_id=(peer(k), t), device_id_type=MESH)

    def block_chip(i):
        return jnp.where(low, chips - 1 - i, i)

    blocks = [(n, 0, width) for n in range(members)]
    if pieces % 2 == 0:
        blocks[:1] = [(0, p * width // 2, width // 2) for p in range(2)]
    chunks = len(blocks)
    loaded = set()

    def weight_copy(j):
        n, offset, size = blocks[j]
        column = block_chip(n % chips) * 2 + n // chips
        start = pl.multiple_of(column * width + offset, LANES)
        return pltpu.make_async_copy(
            w_ref.at[:, pl.ds(start, size)], wbuf.at[n, :, pl.ds(offset, size)],
            w_sem.at[j % AHEAD],
        )

    def weights(n, column):
        for j in range(chunks):
            if j not in loaded and blocks[j][:2] <= (n, column) and blocks[j][0] == n:
                weight_copy(j).wait()
                loaded.add(j)
                if j + AHEAD < chunks:
                    weight_copy(j + AHEAD).start()

    down_copy = pltpu.make_async_copy(down_ref, dbuf, d_sem.at[0])
    up_copy = pltpu.make_async_copy(up_ref, ubuf, d_sem.at[1])
    res_copy = pltpu.make_async_copy(res_ref, rbuf, d_sem.at[2])
    x_copy = pltpu.make_async_copy(x_hbm, x_ref, d_sem.at[0])
    idx_copy = pltpu.make_async_copy(idx_hbm, idx_ref, d_sem.at[1])
    idx_copy.start()
    x_copy.start()
    for j in range(min(FIRST, chunks)):
        weight_copy(j).start()

    def enter():
        near_chips = jnp.where(z > 0, 1, 0) + jnp.where(z < last_chip, 1, 0)
        pl.semaphore_wait(barrier, 1 + len(near) + near_chips)

    def tell(b):
        pl.semaphore_signal(
            dp_sem.at[b], inc=1, device_id=(peer(1 << b), t), device_id_type=MESH
        )

    def tell_chip(n, to):
        pl.semaphore_signal(z_sem.at[n], inc=1, device_id=core_of(to), device_id_type=MESH)

    def greet_far():
        for b in range(rounds):
            pl.semaphore_wait(dp_sem.at[b], 1)
            if b + 1 < rounds:
                tell(b + 1)

    def greet_ends():
        if chips < 3:
            return

        @pl.when(z == 0)
        def _():
            tell_chip(0, z + 1)

        @pl.when(z == last_chip)
        def _():
            tell_chip(1, z - 1)

    def greet_chips():
        if chips < 3:
            return

        @pl.when((z > 0) & low)
        def _():
            pl.semaphore_wait(z_sem.at[0], 1)
            tell_chip(0, z + 1)
            pl.semaphore_wait(z_sem.at[1], 1)
            tell_chip(1, z - 1)

        @pl.when((z < last_chip) & jnp.logical_not(low))
        def _():
            pl.semaphore_wait(z_sem.at[1], 1)
            tell_chip(1, z - 1)
            pl.semaphore_wait(z_sem.at[0], 1)
            tell_chip(0, z + 1)

    def meet_chips():
        if chips < 3:
            return

        @pl.when(z == 0)
        def _():
            pl.semaphore_wait(z_sem.at[1], 1)

        @pl.when(z == last_chip)
        def _():
            pl.semaphore_wait(z_sem.at[0], 1)

    idx_copy.wait()
    for j in range(FIRST, min(AHEAD, chunks)):
        weight_copy(j).start()
    idx_row = idx_ref[...]
    r_i = lax.broadcasted_iota(jnp.int32, (rows, rows), 0)
    c_i = lax.broadcasted_iota(jnp.int32, (rows, rows), 1)
    idx_full = jnp.broadcast_to(idx_row, (rows, rows))
    idx_col = jnp.sum(jnp.where(r_i == c_i, idx_full, 0), axis=1, keepdims=True)
    own_row = idx_row // owned
    own_col = idx_col // owned
    same = own_col == own_row
    rank_row = jnp.sum(jnp.where(same & (r_i < c_i), 1, 0), axis=0, keepdims=True)
    rank_col = jnp.sum(jnp.where(same & (c_i < r_i), 1, 0), axis=1, keepdims=True)

    def slot_of(place_rank, owner, h):
        inside = place_rank - h * part
        keep = (inside >= 0) & (inside < part)
        return jnp.where(keep, owner * part + inside, -1)

    number_row = lax.rem(idx_row, owned) + 1
    step = min(256, depth)

    def row_copy(h, k):
        to = peer(k)
        return pltpu.make_async_remote_copy(
            src_ref=xsend.at[h, to], dst_ref=xrecv.at[h, g],
            send_sem=xs_sem.at[0], recv_sem=xr_sem.at[h],
            device_id=(to, t), device_id_type=MESH,
        )

    others = pl.ds(0, groups - 1)

    def all_of(send, recv, send_sem, recv_sem):
        return pltpu.make_async_remote_copy(
            src_ref=send, dst_ref=recv, send_sem=send_sem, recv_sem=recv_sem,
            device_id=(g, partner), device_id_type=MESH,
        )

    def rows_wait(h):
        all_of(
            xsend.at[h, others], xrecv.at[h, others], xs_sem.at[0], xr_sem.at[h]
        ).wait_recv()

    def place_rows(h):
        slot_row = slot_of(rank_row, own_row, h)
        placing = lax.broadcasted_iota(jnp.int32, (slots, rows), 0) == slot_row
        request = jnp.sum(jnp.where(placing, number_row, 0), axis=1, keepdims=True)
        place = jnp.where(placing, 1.0, 0.0).astype(BF16)
        numbers = jnp.broadcast_to(request.astype(F32), (slots, LANES)).astype(BF16)
        for k in range(groups):
            xsend[h, k, :, depth:] = numbers[k * part:(k + 1) * part]
        for j in range(depth // step):
            moved = jnp.dot(
                place, x_ref[:, j * step:(j + 1) * step], preferred_element_type=F32
            ).astype(BF16)
            for k in range(groups):
                xsend[h, k, :, j * step:(j + 1) * step] = moved[k * part:(k + 1) * part]
        xrecv[h, g] = xsend[h, g]

    tile = min(256, piece)
    tiles = piece // tile

    def pair_copy(chip, q):
        k = chip * pieces + q
        return pltpu.make_async_remote_copy(
            src_ref=psend.at[k], dst_ref=precv.at[k], send_sem=ps_sem.at[0],
            recv_sem=pr_sem.at[k], device_id=(g, partner), device_id_type=MESH,
        )

    strip = 16

    def hop(chip, q, to, send, recv, s_sem, shift):
        k = chip * pieces + q
        return pltpu.make_async_remote_copy(
            src_ref=send.at[k], dst_ref=recv.at[k], send_sem=s_sem.at[0],
            recv_sem=hr_sem.at[k + shift * pieces], device_id=(g, to * 2 + c),
            device_id_type=MESH,
        )

    right = functools.partial(hop, send=rsend, recv=rrecv, s_sem=rs_sem, shift=1)
    left = functools.partial(hop, send=lsend, recv=lrecv, s_sem=ls_sem, shift=0)

    def pass_on(chip, q, first, to, make, send, recv):
        k = chip * pieces + q
        if not first:
            make(chip, q, to).wait_recv()

        @pl.loop(0, rows // strip)
        def _(n):
            at = pl.ds(pl.multiple_of(n * strip, strip), strip)
            value = own[k, at] + precv[k, at].astype(F32)
            if not first:
                value = value + recv[k, at].astype(F32)
            send[k, at] = value.astype(BF16)

        make(chip, q, to).start()

    sent = set()

    def send_first(core, turn, q):
        if turn >= last_chip or ("first", core, turn, q) in sent:
            return
        sent.add(("first", core, turn, q))

        @pl.when((c == core) & (z == 0))
        def _():
            pass_on(chips - 1 - turn, q, True, z + 1, right, rsend, rrecv)

        @pl.when((c == core) & (z == last_chip))
        def _():
            pass_on(turn, q, True, z - 1, left, lsend, lrecv)

    def send_on(core, turn, q):
        if turn == 0 or turn >= last_chip or ("on", core, turn, q) in sent:
            return
        sent.add(("on", core, turn, q))

        @pl.when((c == core) & (z > 0) & (z <= turn))
        def _():
            pass_on(chips - 1 - turn + z, q, False, z + 1, right, rsend, rrecv)

        @pl.when((c == core) & (z < last_chip) & (last_chip - z <= turn))
        def _():
            pass_on(turn - chips + 1 + z, q, False, z - 1, left, lsend, lrecv)

    wave = 2 if pieces % 2 == 0 else 1

    steps = [(i, q) for i in range(chips) for q in range(0, pieces, wave)]

    def product(n, q, into, k):
        for m in range(tiles * wave):
            at = q * piece + m * tile
            into[k + m // tiles, :, m % tiles * tile:(m % tiles + 1) * tile] = jnp.dot(
                x_ref[...], wbuf[n, :, at:at + tile], preferred_element_type=F32
            ).astype(into.dtype)

    def project(phase, n):
        i, q = steps[n]
        block = phase * chips + i
        k = block_chip(i) * pieces + q
        weights(block, q * piece)

        @pl.when(c == phase)
        def _():
            product(block, q, own, k)

        @pl.when(c != phase)
        def _():
            product(block, q, psend, k)
            if phase + n > 0:
                send_other(n)

    def send_other(n):
        i, q = steps[n]
        for p in range(wave):
            pair_copy(block_chip(i), q + p).start()

    def settle(phase, n):
        i, first = steps[n]
        for q in range(first, first + wave):
            @pl.when(c == phase)
            def _():
                pair_copy(block_chip(i), q).wait_recv()

            if phase == 0:
                send_first(0, i, q)

    lane_number = (lax.broadcasted_iota(jnp.int32, (slots, LANES), 1) // rank + 1).astype(F32)
    per_tile = LANES // rank
    tile_count = owned * rank // LANES
    chunk = min(512, owned * rank)

    def term_pair(h):
        return pltpu.make_async_remote_copy(
            src_ref=packed.at[h], dst_ref=arp.at[h], send_sem=as_sem.at[0],
            recv_sem=ar_sem.at[h], device_id=(g, partner), device_id_type=MESH,
        )

    def term_copy(h, k, core):
        to = lax.rem(z + k, chips)
        return pltpu.make_async_remote_copy(
            src_ref=arz.at[h, z], dst_ref=arz.at[h, z], send_sem=zs_sem.at[0],
            recv_sem=zr_sem.at[h], device_id=(g, to * 2 + core), device_id_type=MESH,
        )

    def terms_wait(h):
        @pl.when(c == 0)
        def _():
            all_of(arz.at[h], arz.at[h], zs_sem.at[0], zr_sem.at[h]).wait_recv()

        if chips > 1:
            @pl.when(c == 1)
            def _():
                far_chips = pl.ds(0, chips - 1)
                all_of(
                    arz.at[h, far_chips], arz.at[h, far_chips], zs_sem.at[0], zr_sem.at[h]
                ).wait_recv()

    def wanted_of(h):
        return xrecv[h, :, :, depth:].reshape(slots, LANES).astype(F32)

    def shrink_rows(h):
        rows_wait(h)
        if h == 0:
            down_copy.wait()
        wanted = wanted_of(h).T[:rank]
        flat = xrecv[h, :, :, :depth].reshape(slots, depth)
        mine = jnp.zeros((rank, slots), F32)
        for first in range(0, owned * rank, chunk):
            every = lax.dot_general(
                dbuf[first:first + chunk, :], flat, (((1,), (1,)), ((), ())),
                preferred_element_type=F32,
            )
            for p in range(chunk // rank):
                number = float(first // rank + p + 1)
                mine = jnp.where(wanted == number, every[p * rank:(p + 1) * rank], mine)
        packed[h] = mine

        @pl.when(c == 0)
        def _():
            term_pair(h).start()

    def sum_send(h):
        @pl.when(c == 1)
        def _():
            term_pair(h).wait_recv()
            arz[h, z] = packed[h] + arp[h]
            term_copy(h, 0, 0).start()
            for k in range(1, chips):
                for core in range(2):
                    term_copy(h, k, core).start()

    def back_copy(h, k):
        to = peer(k)
        return pltpu.make_async_remote_copy(
            src_ref=esend.at[h, to], dst_ref=eback.at[h, g],
            send_sem=es_sem.at[0], recv_sem=er_sem.at[h],
            device_id=(to, t), device_id_type=MESH,
        )

    def back_wait(h):
        all_of(
            esend.at[h, others], eback.at[h, others], es_sem.at[0], er_sem.at[h]
        ).wait_recv()

    wide = min(256, width)

    def expand_rows(h):
        terms_wait(h)
        total = arz[h, 0]
        for k in range(1, chips):
            total = total + arz[h, k]
        total = total.astype(BF16).astype(F32)
        if h == 0:
            up_copy.wait()
        wanted = wanted_of(h)
        shrink = jnp.concatenate([total] * per_tile, axis=0).T
        spread = jnp.concatenate(
            [
                jnp.where(wanted == lane_number + float(m * per_tile), shrink, 0.0).astype(BF16)
                for m in range(tile_count)
            ],
            axis=1,
        )

        @pl.loop(0, width // wide)
        def _(n):
            cols = pl.ds(pl.multiple_of(n * wide, LANES), wide)
            grown = jnp.dot(spread, ubuf[:, cols], preferred_element_type=F32).astype(BF16)
            for k in range(groups):
                esend[h, k, :, cols] = grown[k * part:(k + 1) * part]

        for k in range(1, groups):
            back_copy(h, k).start()
        eback[h, g] = esend[h, g]

    with scope("x"):
        x_copy.wait()
    with scope("place0"):
        place_rows(0)
    with scope("project0_0"):
        project(0, 0)
    with scope("enter"):
        enter()

    @pl.when(c == 1)
    def _():
        send_other(0)

    if rounds:
        tell(0)
    greet_ends()

    def near_rows(h):
        for k in near:
            row_copy(h, k).start()

    def far_rows(h):
        if h == 0:
            greet_far()
        for k in far:
            row_copy(h, k).start()

    def load_factors():
        down_copy.start()
        up_copy.start()
        res_copy.start()

    stages = {
        "project": project, "settle": settle, "place": place_rows, "near": near_rows,
        "far": far_rows, "greet": greet_chips, "meet": meet_chips, "factors": load_factors,
        "shrink": shrink_rows, "sum": sum_send, "expand": expand_rows,
        "first": send_first, "on": send_on,
    }
    for name, *at in ORDER:
        if name in ("first", "on"):
            if at[2] >= pieces:
                continue
        elif name in ("project", "settle"):
            if at[1] >= len(steps):
                continue
        elif at and at[0] >= halves:
            continue
        with scope(name + "_".join(str(v) for v in at)):
            stages[name](*at)
    for turn in range(last_chip):
        for q in range(pieces):
            for core in range(2):
                send_first(core, turn, q)
                send_on(core, turn, q)

    res_copy.wait()

    def branch_of(h, q, n):
        slot_col = slot_of(rank_col, own_col, h)
        unplace = jnp.where(
            lax.broadcasted_iota(jnp.int32, (rows, slots), 1) == slot_col, 1.0, 0.0
        ).astype(BF16)
        first = q * piece + n * tile
        back = eback[h, :, :, first:first + tile].reshape(slots, tile)
        return jnp.dot(unplace, back, preferred_element_type=F32)

    for h in range(halves):
        with scope("backwait%d" % h):
            back_wait(h)
        for q in range(pieces):
            for n in range(tiles):
                cols = slice(n * tile, (n + 1) * tile)
                first = q * piece + n * tile
                value = own[z * pieces + q, :, cols] + branch_of(h, q, n)
                if h == 0:
                    value = (
                        value + precv[z * pieces + q, :, cols].astype(F32)
                        + rbuf[:, first:first + tile].astype(F32)
                    )
                own[z * pieces + q, :, cols] = value

    for q in range(pieces):
        mine_at = z * pieces + q
        mark = scope("fin%d" % q)
        mark.__enter__()

        def finish(use_right, use_left):
            @pl.loop(0, rows // strip)
            def _(n):
                at = pl.ds(pl.multiple_of(n * strip, strip), strip)
                value = own[mine_at, at]
                if use_right:
                    value = value + rrecv[mine_at, at].astype(F32)
                if use_left:
                    value = value + lrecv[mine_at, at].astype(F32)
                out_ref[at, q * piece:(q + 1) * piece] = value.astype(BF16)

        if chips == 1:
            finish(False, False)
        else:
            @pl.when(z == 0)
            def _():
                left(z, q, z).wait_recv()
                finish(False, True)

            @pl.when(z == chips - 1)
            def _():
                right(z, q, z).wait_recv()
                finish(True, False)

            @pl.when((z > 0) & (z < chips - 1))
            def _():
                right(z, q, z).wait_recv()
                left(z, q, z).wait_recv()
                finish(True, True)
        mark.__exit__(None, None, None)

    tail = scope("tail")
    tail.__enter__()
    all_of(psend, precv, ps_sem.at[0], ps_sem.at[0]).wait_send()

    @pl.when(c == 0)
    def _():
        all_of(packed, arp, as_sem.at[0], as_sem.at[0]).wait_send()

    @pl.when(c == 1)
    def _():
        all_of(arz, arz, zs_sem.at[0], zs_sem.at[0]).wait_send()
        if chips > 1:
            far_chips = pl.ds(0, chips - 1)
            all_of(
                arz.at[:, far_chips], arz.at[:, far_chips], zs_sem.at[0], zs_sem.at[0]
            ).wait_send()

    if groups > 1:
        all_of(
            xsend.at[:, others], xrecv.at[:, others], xs_sem.at[0], xs_sem.at[0]
        ).wait_send()
        all_of(
            esend.at[:, others], eback.at[:, others], es_sem.at[0], es_sem.at[0]
        ).wait_send()
    for chip in range(chips):
        @pl.when(z == chip)
        def _():
            if chip < last_chip:
                sent = pl.ds(0, (last_chip - chip) * pieces)
                all_of(
                    rsend.at[sent], rrecv.at[sent], rs_sem.at[0], rs_sem.at[0]
                ).wait_send()
            if chip > 0:
                sent = pl.ds(0, chip * pieces)
                all_of(
                    lsend.at[sent], lrecv.at[sent], ls_sem.at[0], ls_sem.at[0]
                ).wait_send()
    tail.__exit__(None, None, None)


def body(attention_output, residual, output_weight, down_factors, up_factors, adapter_index):
    groups = lax.axis_size("dp")
    members = lax.axis_size("tensor")
    rows, depth = attention_output.shape
    owned, _, rank = down_factors.shape
    width = output_weight.shape[1] // members
    cap = 2 * rows // groups
    chips = members // 2
    halves = 2 if cap % 32 == 0 else 1
    part = cap // halves
    slots = groups * part
    pieces = max(1, min(PIECES, width // 256))
    piece = width // pieces
    down = jnp.swapaxes(down_factors, 1, 2).reshape(owned * rank, depth)
    up = up_factors.reshape(owned * rank, width)
    vmem = pl.BlockSpec(memory_space=pltpu.VMEM)
    hbm = pl.BlockSpec(memory_space=pl.ANY)
    dma = pltpu.SemaphoreType.DMA
    hops = chips * pieces
    return pl.pallas_call(
        functools.partial(kernel, groups, members, rank, owned, halves, pieces),
        out_shape=pltpu.VMEM((rows, width), BF16),
        in_specs=[hbm] * 6,
        out_specs=vmem,
        scratch_shapes=[
            pltpu.VMEM((rows, depth), BF16),
            pltpu.VMEM((1, rows), jnp.int32),
            pltpu.VMEM((members, depth, width), BF16),
            pltpu.VMEM((owned * rank, depth), BF16),
            pltpu.VMEM((owned * rank, width), BF16),
            pltpu.VMEM((rows, width), BF16),
            pltpu.VMEM((hops, rows, piece), F32),
            pltpu.VMEM((hops, rows, piece), BF16),
            pltpu.VMEM((hops, rows, piece), BF16),
            pltpu.VMEM((hops, rows, piece), BF16),
            pltpu.VMEM((hops, rows, piece), BF16),
            pltpu.VMEM((hops, rows, piece), BF16),
            pltpu.VMEM((hops, rows, piece), BF16),
            pltpu.VMEM((halves, groups, part, depth + LANES), BF16),
            pltpu.VMEM((halves, groups, part, depth + LANES), BF16),
            pltpu.VMEM((halves, rank, slots), F32),
            pltpu.VMEM((halves, rank, slots), F32),
            pltpu.VMEM((halves, chips, rank, slots), F32),
            pltpu.VMEM((halves, groups, part, width), BF16),
            pltpu.VMEM((halves, groups, part, width), BF16),
            dma((AHEAD,)), dma((3,)), dma((1,)), dma((hops,)),
            dma((1,)), dma((1,)), dma((hops + pieces,)),
            dma((1,)), dma((halves,)), dma((1,)), dma((halves,)),
            dma((1,)), dma((halves,)), dma((1,)), dma((halves,)),
            pltpu.SemaphoreType.REGULAR((max(1, groups.bit_length() - 2),)),
            pltpu.SemaphoreType.REGULAR((2,)),
        ],
        compiler_params=pltpu.CompilerParams(
            collective_id=0, has_side_effects=True, vmem_limit_bytes=60 * 1024 * 1024
        ),
    )(attention_output, residual, adapter_index.reshape(1, rows), output_weight, down, up)


def solution(mesh):
    return jax.shard_map(
        body,
        mesh=mesh,
        in_specs=(
            P("dp", "tensor"),
            P("dp", "tensor"),
            P("tensor", None),
            P("dp", "tensor", None),
            P("dp", None, "tensor"),
            P("dp"),
        ),
        out_specs=P("dp", "tensor"),
        check_vma=False,
    )
```

time: 34.1 us -> 29.5 us (0.87)
  Pallas kernels: 32.2 us -> 28.7 us
  local copies, waits for them, and re-layouts: 1.67 us -> 0.71 us
    pallas_call x1, Pallas kernels: 32.2 us -> 28.7 us  [body(): pl.pallas_call(functools.partial(kernel, groups, members, rank, owned, ha...]
    unnamed x1, local copies, waits for them, and re-layouts: 1.67 us -> 0.71 us
where the time goes in v1:
time: 29.5 us; the launch traced here: 29.4 us
  Pallas kernels  28.7 us (97%)
  local copies, waits for them, and re-layouts  0.71 us (2%)
    pallas_call x1, Pallas kernels, body(): pl.pallas_call(functools.partial(kernel, groups, members, rank, owned, ha...  28.7 us
    unnamed x1, local copies, waits for them, and re-layouts  0.71 us

profile of v1, /device:TPU:0, one launch (start us, length us, event | category | flops | bytes accessed | tf_op | source)
XLA Modules:
  0.0 29.4 jit_solution(9514819229178289106)
XLA Ops:
  0.0 28.7 %shard_map.64 = bf16[128,1024]{1,0:T(8,128)(2,1)S(1)} custom-call(bf16[128,1024]{1,0:T(8,128)(2,1)} %x_hbm.1, bf16[128,1024]{1,0:T(8,128)(2,1)} %res_ref.1, s32[1,128]{1,0:T(1,128)} %bitcast.7, bf16[1024,8192]{1,0:T(8,128)(2,1)} %w_ref.1, bf16[1024,1024]{1,0:T(8,128)(2,1)} %bitcast.5, bf16[1024,1024]{1,0:T(8,128)(2,1)} %bitcast.6), custom_call_target="tpu_custom_call" | custom-call | tf_op jit(solution)/shard_map/pallas_call | solution.py:650
  28.7 0.7 %copy.8 = bf16[128,1024]{1,0:T(8,128)(2,1)} copy(bf16[128,1024]{1,0:T(8,128)(2,1)S(1)} %shard_map.64) | data formatting | bytes 524288

commit v2 on v1

--- a/solution.py
+++ b/solution.py
@@ -17,26 +17,28 @@
 FIRST = 2
 ORDER = (
     ("near", 0), ("project", 0, 1), ("project", 0, 2), ("settle", 0, 0), ("far", 0),
-    ("project", 0, 3), ("settle", 0, 1), ("place", 1), ("near", 1), ("far", 1), ("factors",),
+    ("project", 0, 3), ("settle", 0, 1), ("place", 1), ("far", 1), ("near", 1), ("factors",),
     ("project", 0, 4), ("settle", 0, 2), ("project", 0, 5), ("settle", 0, 3),
     ("project", 0, 6), ("settle", 0, 4), ("project", 0, 7), ("settle", 0, 5),
-    ("project", 1, 0), ("settle", 0, 6), ("project", 1, 1), ("settle", 0, 7), ("greet",),
-    ("project", 1, 2), ("on", 0, 1, 0), ("on", 0, 1, 1),
-    ("shrink", 0), ("project", 1, 3), ("project", 1, 4), ("meet",), ("sum", 0),
-    ("on", 0, 1, 2), ("on", 0, 1, 3),
-    ("project", 1, 5), ("settle", 1, 0), ("settle", 1, 1),
-    ("first", 1, 0, 0), ("first", 1, 0, 1), ("first", 1, 0, 2),
-    ("project", 1, 6), ("project", 1, 7),
-    ("shrink", 1), ("on", 0, 2, 0), ("on", 0, 2, 1), ("sum", 1),
-    ("settle", 1, 2), ("settle", 1, 3), ("settle", 1, 4), ("settle", 1, 5),
+    ("project", 1, 0), ("settle", 0, 6), ("settle", 0, 7), ("requests",), ("greet",),
+    ("on", 0, 1, 0), ("on", 0, 1, 1), ("on", 0, 1, 2), ("on", 0, 1, 3),
+    ("shrink", 0), ("project", 1, 1), ("project", 1, 2),
+    ("meet",), ("sum", 0), ("project", 1, 3),
+    ("settle", 1, 0), ("settle", 1, 1), ("first", 1, 0, 0),
+    ("shrink", 1), ("project", 1, 4), ("sum", 1),
+    ("first", 1, 0, 1), ("first", 1, 0, 2), ("first", 1, 0, 3),
+    ("project", 1, 5), ("project", 1, 6), ("project", 1, 7),
+    ("settle", 1, 2), ("settle", 1, 3),
+    ("first", 1, 1, 0), ("first", 1, 1, 1), ("first", 1, 1, 2), ("first", 1, 1, 3),
+    ("settle", 1, 4), ("settle", 1, 5),
+    ("first", 1, 2, 0), ("first", 1, 2, 1), ("first", 1, 2, 2), ("first", 1, 2, 3),
     ("settle", 1, 6), ("settle", 1, 7),
-    ("first", 1, 0, 3),
-    ("first", 1, 1, 0), ("first", 1, 1, 1), ("first", 1, 1, 2), ("first", 1, 1, 3),
-    ("first", 1, 2, 0), ("first", 1, 2, 1), ("first", 1, 2, 2), ("first", 1, 2, 3),
-    ("on", 0, 2, 2), ("on", 0, 2, 3),
-    ("expand", 0), ("on", 1, 1, 0), ("expand", 1),
-    ("on", 1, 1, 1), ("on", 1, 1, 2), ("on", 1, 1, 3),
-    ("on", 1, 2, 0), ("on", 1, 2, 1), ("on", 1, 2, 2), ("on", 1, 2, 3),
+    ("on", 0, 2, 0), ("on", 0, 2, 1), ("on", 0, 2, 2), ("on", 0, 2, 3),
+    ("long", 0, 2, 0), ("long", 0, 2, 1), ("on", 1, 1, 0),
+    ("expand", 0), ("long", 0, 2, 2), ("long", 0, 2, 3),
+    ("on", 1, 1, 1), ("on", 1, 1, 2), ("on", 1, 1, 3), ("expand", 1),
+    ("long", 1, 2, 0), ("on", 1, 2, 0), ("long", 1, 2, 1), ("on", 1, 2, 1),
+    ("long", 1, 2, 2), ("on", 1, 2, 2), ("long", 1, 2, 3), ("on", 1, 2, 3),
 )
 scope = contextlib.nullcontext
 
@@ -44,10 +46,10 @@
 def kernel(
     groups, members, rank, owned, halves, pieces,
     x_hbm, res_ref, idx_hbm, w_ref, down_ref, up_ref, out_ref,
-    x_ref, idx_ref, wbuf, dbuf, ubuf, rbuf, own, psend, precv, rrecv, lrecv, rsend, lsend,
-    xsend, xrecv, packed, arp, arz, esend, eback,
+    x_ref, idx_ref, idx_all, wbuf, dbuf, ubuf, rbuf, own, psend, precv, rrecv, lrecv, rsend, lsend,
+    xsend, xrecv, wants, packed, arp, arz, esend, eback,
     w_sem, d_sem, ps_sem, pr_sem, rs_sem, ls_sem, hr_sem,
-    xs_sem, xr_sem, as_sem, ar_sem, zs_sem, zr_sem, es_sem, er_sem, dp_sem, z_sem,
+    xs_sem, xr_sem, as_sem, ar_sem, zs_sem, zr_sem, es_sem, er_sem, dp_sem, z_sem, is_sem, ir_sem,
 ):
     chips = members // 2
     g = lax.axis_index("dp")
@@ -60,6 +62,7 @@
     part = xrecv.shape[2]
     slots = groups * part
     low = z < chips // 2
+    high = jnp.logical_not(low)
     piece = width // pieces
     last_chip = chips - 1
 
@@ -214,7 +217,6 @@
         keep = (inside >= 0) & (inside < part)
         return jnp.where(keep, owner * part + inside, -1)
 
-    number_row = lax.rem(idx_row, owned) + 1
     step = min(256, depth)
 
     def row_copy(h, k):
@@ -233,6 +235,34 @@
             device_id=(g, partner), device_id_type=MESH,
         )
 
+    def idx_copy_to(k):
+        return pltpu.make_async_remote_copy(
+            src_ref=idx_ref, dst_ref=idx_all.at[g], send_sem=is_sem.at[0],
+            recv_sem=ir_sem.at[0], device_id=(peer(k), t), device_id_type=MESH,
+        )
+
+    def requests():
+        idx_all[g] = idx_ref[...]
+        if groups > 1:
+            all_of(
+                idx_all.at[others], idx_all.at[others], is_sem.at[0], ir_sem.at[0]
+            ).wait_recv()
+        every_row = jnp.concatenate([idx_all[k] for k in range(groups)], axis=0)
+        chosen = every_row // owned == g
+        earlier = jnp.where(r_i < c_i, 1.0, 0.0).astype(BF16)
+        ahead = jnp.dot(
+            jnp.where(chosen, 1.0, 0.0).astype(BF16), earlier, preferred_element_type=F32
+        ).astype(jnp.int32)
+        slot = jnp.where(chosen, ahead, -1)
+        number = lax.rem(every_row, owned) + 1
+        for h in range(halves):
+            for k in range(groups):
+                place = lax.broadcasted_iota(jnp.int32, (part, rows), 0) + h * part
+                asked = jnp.where(place == slot[k:k + 1], number[k:k + 1], 0)
+                wants[h, k * part:(k + 1) * part] = jnp.broadcast_to(
+                    jnp.sum(asked, axis=1, keepdims=True).astype(F32), (part, LANES)
+                )
+
     def rows_wait(h):
         all_of(
             xsend.at[h, others], xrecv.at[h, others], xs_sem.at[0], xr_sem.at[h]
@@ -241,11 +271,7 @@
     def place_rows(h):
         slot_row = slot_of(rank_row, own_row, h)
         placing = lax.broadcasted_iota(jnp.int32, (slots, rows), 0) == slot_row
-        request = jnp.sum(jnp.where(placing, number_row, 0), axis=1, keepdims=True)
         place = jnp.where(placing, 1.0, 0.0).astype(BF16)
-        numbers = jnp.broadcast_to(request.astype(F32), (slots, LANES)).astype(BF16)
-        for k in range(groups):
-            xsend[h, k, :, depth:] = numbers[k * part:(k + 1) * part]
         for j in range(depth // step):
             moved = jnp.dot(
                 place, x_ref[:, j * step:(j + 1) * step], preferred_element_type=F32
@@ -312,11 +338,24 @@
             return
         sent.add(("on", core, turn, q))
 
-        @pl.when((c == core) & (z > 0) & (z <= turn))
+        @pl.when((c == core) & low & (z > 0) & (z <= turn))
         def _():
             pass_on(chips - 1 - turn + z, q, False, z + 1, right, rsend, rrecv)
 
-        @pl.when((c == core) & (z < last_chip) & (last_chip - z <= turn))
+        @pl.when((c == core) & high & (z < last_chip) & (last_chip - z <= turn))
+        def _():
+            pass_on(turn - chips + 1 + z, q, False, z - 1, left, lsend, lrecv)
+
+    def send_long(core, turn, q):
+        if turn < chips - chips // 2 or turn >= last_chip or ("long", core, turn, q) in sent:
+            return
+        sent.add(("long", core, turn, q))
+
+        @pl.when((c == core) & high & (z <= turn))
+        def _():
+            pass_on(chips - 1 - turn + z, q, False, z + 1, right, rsend, rrecv)
+
+        @pl.when((c == core) & low & (last_chip - z <= turn))
         def _():
             pass_on(turn - chips + 1 + z, q, False, z - 1, left, lsend, lrecv)
 
@@ -374,7 +413,7 @@
         )
 
     def term_copy(h, k, core):
-        to = lax.rem(z + k, chips)
+        to = lax.rem(z + jnp.where(low, chips - k, k), chips)
         return pltpu.make_async_remote_copy(
             src_ref=arz.at[h, z], dst_ref=arz.at[h, z], send_sem=zs_sem.at[0],
             recv_sem=zr_sem.at[h], device_id=(g, to * 2 + core), device_id_type=MESH,
@@ -394,14 +433,14 @@
                 ).wait_recv()
 
     def wanted_of(h):
-        return xrecv[h, :, :, depth:].reshape(slots, LANES).astype(F32)
+        return wants[h]
 
     def shrink_rows(h):
         rows_wait(h)
         if h == 0:
             down_copy.wait()
         wanted = wanted_of(h).T[:rank]
-        flat = xrecv[h, :, :, :depth].reshape(slots, depth)
+        flat = xrecv[h].reshape(slots, depth)
         mine = jnp.zeros((rank, slots), F32)
         for first in range(0, owned * rank, chunk):
             every = lax.dot_general(
@@ -440,7 +479,7 @@
             esend.at[h, others], eback.at[h, others], es_sem.at[0], er_sem.at[h]
         ).wait_recv()
 
-    wide = min(256, width)
+    wide = min(512, width)
 
     def expand_rows(h):
         terms_wait(h)
@@ -467,7 +506,7 @@
             for k in range(groups):
                 esend[h, k, :, cols] = grown[k * part:(k + 1) * part]
 
-        for k in range(1, groups):
+        for k in far + near:
             back_copy(h, k).start()
         eback[h, g] = esend[h, g]
 
@@ -490,12 +529,16 @@
 
     def near_rows(h):
         for k in near:
+            if h == 0:
+                idx_copy_to(k).start()
             row_copy(h, k).start()
 
     def far_rows(h):
         if h == 0:
             greet_far()
         for k in far:
+            if h == 0:
+                idx_copy_to(k).start()
             row_copy(h, k).start()
 
     def load_factors():
@@ -507,10 +550,10 @@
         "project": project, "settle": settle, "place": place_rows, "near": near_rows,
         "far": far_rows, "greet": greet_chips, "meet": meet_chips, "factors": load_factors,
         "shrink": shrink_rows, "sum": sum_send, "expand": expand_rows,
-        "first": send_first, "on": send_on,
+        "first": send_first, "on": send_on, "long": send_long, "requests": requests,
     }
     for name, *at in ORDER:
-        if name in ("first", "on"):
+        if name in ("first", "on", "long"):
             if at[2] >= pieces:
                 continue
         elif name in ("project", "settle"):
@@ -524,6 +567,7 @@
         for q in range(pieces):
             for core in range(2):
                 send_first(core, turn, q)
+                send_long(core, turn, q)
                 send_on(core, turn, q)
 
     res_copy.wait()
@@ -612,6 +656,7 @@
         all_of(
             esend.at[:, others], eback.at[:, others], es_sem.at[0], es_sem.at[0]
         ).wait_send()
+        all_of(idx_all.at[others], idx_all.at[others], is_sem.at[0], is_sem.at[0]).wait_send()
     for chip in range(chips):
         @pl.when(z == chip)
         def _():
@@ -655,6 +700,7 @@
         scratch_shapes=[
             pltpu.VMEM((rows, depth), BF16),
             pltpu.VMEM((1, rows), jnp.int32),
+            pltpu.VMEM((groups, 1, rows), jnp.int32),
             pltpu.VMEM((members, depth, width), BF16),
             pltpu.VMEM((owned * rank, depth), BF16),
             pltpu.VMEM((owned * rank, width), BF16),
@@ -666,8 +712,9 @@
             pltpu.VMEM((hops, rows, piece), BF16),
             pltpu.VMEM((hops, rows, piece), BF16),
             pltpu.VMEM((hops, rows, piece), BF16),
-            pltpu.VMEM((halves, groups, part, depth + LANES), BF16),
-            pltpu.VMEM((halves, groups, part, depth + LANES), BF16),
+            pltpu.VMEM((halves, groups, part, depth), BF16),
+            pltpu.VMEM((halves, groups, part, depth), BF16),
+            pltpu.VMEM((halves, slots, LANES), F32),
             pltpu.VMEM((halves, rank, slots), F32),
             pltpu.VMEM((halves, rank, slots), F32),
             pltpu.VMEM((halves, chips, rank, slots), F32),
@@ -679,6 +726,7 @@
             dma((1,)), dma((halves,)), dma((1,)), dma((halves,)),
             pltpu.SemaphoreType.REGULAR((max(1, groups.bit_length() - 2),)),
             pltpu.SemaphoreType.REGULAR((2,)),
+            dma((1,)), dma((1,)),
         ],
         compiler_params=pltpu.CompilerParams(
             collective_id=0, has_side_effects=True, vmem_limit_bytes=60 * 1024 * 1024

time: 29.5 us -> 27.5 us (0.932)
  the two profiles are of different devices: /device:TPU:0 before, /device:TPU:1 now
where the time goes in v2:
time: 27.5 us; the launch traced here: 27.3 us
  Pallas kernels  26.6 us (97%)
  local copies, waits for them, and re-layouts  0.71 us (3%)
    pallas_call x1, Pallas kernels, body(): pl.pallas_call(functools.partial(kernel, groups, members, rank, owned, ha...  26.6 us
    unnamed x1, local copies, waits for them, and re-layouts  0.71 us

profile of v2, /device:TPU:1, one launch (start us, length us, event | category | flops | bytes accessed | tf_op | source)
XLA Modules:
  0.0 27.3 jit_solution(17366315739902092616)
XLA Ops:
  0.0 26.6 %shard_map.64 = bf16[128,1024]{1,0:T(8,128)(2,1)S(1)} custom-call(bf16[128,1024]{1,0:T(8,128)(2,1)} %x_hbm.1, bf16[128,1024]{1,0:T(8,128)(2,1)} %res_ref.1, s32[1,128]{1,0:T(1,128)} %bitcast.7, bf16[1024,8192]{1,0:T(8,128)(2,1)} %w_ref.1, bf16[1024,1024]{1,0:T(8,128)(2,1)} %bitcast.5, bf16[1024,1024]{1,0:T(8,128)(2,1)} %bitcast.6), custom_call_target="tpu_custom_call" | custom-call | tf_op jit(solution)/shard_map/pallas_call | solution.py:695
  26.6 0.7 %copy.8 = bf16[128,1024]{1,0:T(8,128)(2,1)} copy(bf16[128,1024]{1,0:T(8,128)(2,1)S(1)} %shard_map.64) | data formatting | bytes 524288

commit v3 on v2

--- a/solution.py
+++ b/solution.py
@@ -15,30 +15,35 @@
 PIECES = 4
 AHEAD = 4
 FIRST = 2
+HELD = 2
 ORDER = (
-    ("near", 0), ("project", 0, 1), ("project", 0, 2), ("settle", 0, 0), ("far", 0),
-    ("project", 0, 3), ("settle", 0, 1), ("place", 1), ("far", 1), ("near", 1), ("factors",),
+    ("near", 0), ("project", 0, 0), ("project", 0, 1), ("project", 0, 2), ("settle", 0, 0),
+    ("far", 0), ("project", 0, 3), ("settle", 0, 1), ("place", 1), ("factors",),
     ("project", 0, 4), ("settle", 0, 2), ("project", 0, 5), ("settle", 0, 3),
-    ("project", 0, 6), ("settle", 0, 4), ("project", 0, 7), ("settle", 0, 5),
-    ("project", 1, 0), ("settle", 0, 6), ("settle", 0, 7), ("requests",), ("greet",),
-    ("on", 0, 1, 0), ("on", 0, 1, 1), ("on", 0, 1, 2), ("on", 0, 1, 3),
-    ("shrink", 0), ("project", 1, 1), ("project", 1, 2),
+    ("far", 1), ("near", 1),
+    ("project", 1, 0), ("project", 0, 6), ("settle", 0, 4), ("greet",), ("project", 0, 7),
+    ("settle", 0, 5), ("settle", 0, 6), ("settle", 0, 7),
+    ("relay", 0, 2, 0), ("relay", 0, 2, 1), ("relay", 0, 2, 2), ("relay", 0, 2, 3),
+    ("requests",), ("relay", 0, 1, 0), ("relay", 0, 1, 1),
+    ("shrink", 0), ("settle", 1, 0), ("first", 1, 0, 0), ("first", 0, 2, 0), ("first", 0, 2, 1),
+    ("relay", 0, 1, 2), ("relay", 0, 1, 3),
+    ("project", 1, 1), ("low", 0, 0), ("low", 0, 1), ("project", 1, 2),
     ("meet",), ("sum", 0), ("project", 1, 3),
-    ("settle", 1, 0), ("settle", 1, 1), ("first", 1, 0, 0),
+    ("first", 1, 0, 1), ("settle", 1, 1), ("first", 1, 0, 2),
     ("shrink", 1), ("project", 1, 4), ("sum", 1),
-    ("first", 1, 0, 1), ("first", 1, 0, 2), ("first", 1, 0, 3),
-    ("project", 1, 5), ("project", 1, 6), ("project", 1, 7),
+    ("low", 0, 2), ("low", 0, 3), ("first", 1, 0, 3), ("project", 1, 5),
+    ("relay", 1, 1, 0), ("project", 1, 6), ("project", 1, 7),
     ("settle", 1, 2), ("settle", 1, 3),
     ("first", 1, 1, 0), ("first", 1, 1, 1), ("first", 1, 1, 2), ("first", 1, 1, 3),
     ("settle", 1, 4), ("settle", 1, 5),
     ("first", 1, 2, 0), ("first", 1, 2, 1), ("first", 1, 2, 2), ("first", 1, 2, 3),
     ("settle", 1, 6), ("settle", 1, 7),
-    ("on", 0, 2, 0), ("on", 0, 2, 1), ("on", 0, 2, 2), ("on", 0, 2, 3),
-    ("long", 0, 2, 0), ("long", 0, 2, 1), ("on", 1, 1, 0),
-    ("expand", 0), ("long", 0, 2, 2), ("long", 0, 2, 3),
-    ("on", 1, 1, 1), ("on", 1, 1, 2), ("on", 1, 1, 3), ("expand", 1),
-    ("long", 1, 2, 0), ("on", 1, 2, 0), ("long", 1, 2, 1), ("on", 1, 2, 1),
-    ("long", 1, 2, 2), ("on", 1, 2, 2), ("long", 1, 2, 3), ("on", 1, 2, 3),
+    ("expand", 0), ("high", 0, 0), ("high", 0, 1), ("high", 0, 2), ("high", 0, 3),
+    ("relay", 1, 1, 1), ("relay", 1, 1, 2),
+    ("relay", 1, 2, 0), ("relay", 1, 2, 1), ("relay", 1, 2, 2), ("relay", 1, 2, 3),
+    ("expand", 1), ("relay", 1, 1, 3), ("first", 0, 2, 2), ("first", 0, 2, 3),
+    ("low", 1, 0), ("high", 1, 0), ("low", 1, 1), ("high", 1, 1),
+    ("low", 1, 2), ("high", 1, 2), ("low", 1, 3), ("high", 1, 3),
 )
 scope = contextlib.nullcontext
 
@@ -46,9 +51,9 @@
 def kernel(
     groups, members, rank, owned, halves, pieces,
     x_hbm, res_ref, idx_hbm, w_ref, down_ref, up_ref, out_ref,
-    x_ref, idx_ref, idx_all, wbuf, dbuf, ubuf, rbuf, own, psend, precv, rrecv, lrecv, rsend, lsend,
+    x_ref, idx_ref, idx_all, wbuf, dbuf, ubuf, rbuf, own, psend, precv, rrecv, lrecv, rsend, lsend, jrecv, klrecv,
     xsend, xrecv, wants, packed, arp, arz, esend, eback,
-    w_sem, d_sem, ps_sem, pr_sem, rs_sem, ls_sem, hr_sem,
+    w_sem, d_sem, ps_sem, pr_sem, rs_sem, ls_sem, hr_sem, j_sem,
     xs_sem, xr_sem, as_sem, ar_sem, zs_sem, zr_sem, es_sem, er_sem, dp_sem, z_sem, is_sem, ir_sem,
 ):
     chips = members // 2
@@ -65,6 +70,7 @@
     high = jnp.logical_not(low)
     piece = width // pieces
     last_chip = chips - 1
+    wave = 2 if pieces % 2 == 0 else 1
 
     def core_of(chip):
         return (g, chip * 2 + c)
@@ -287,79 +293,76 @@
         k = chip * pieces + q
         return pltpu.make_async_remote_copy(
             src_ref=psend.at[k], dst_ref=precv.at[k], send_sem=ps_sem.at[0],
-            recv_sem=pr_sem.at[k], device_id=(g, partner), device_id_type=MESH,
+            recv_sem=pr_sem.at[chip * (pieces // wave) + q // wave],
+            device_id=(g, partner), device_id_type=MESH,
         )
 
     strip = 16
 
-    def hop(chip, q, to, send, recv, s_sem, shift):
-        k = chip * pieces + q
+    sent = set()
+
+    def leaps(core, b):
+        return chips > 2 and b in (0, last_chip)
+
+    def hop(core, a, b, q):
+        k = b * pieces + q
+        to_right = b > a
+        jump = leaps(core, b) and abs(b - a) == 2
+        to = b if jump else (a + 1 if to_right else a - 1)
+        if jump:
+            landing = (jrecv if to_right else klrecv).at[q]
+            arrival = j_sem.at[q + (0 if to_right else pieces)]
+        else:
+            landing = (rrecv if to_right else lrecv).at[k]
+            arrival = hr_sem.at[k + (pieces if to_right else 0)]
         return pltpu.make_async_remote_copy(
-            src_ref=send.at[k], dst_ref=recv.at[k], send_sem=s_sem.at[0],
-            recv_sem=hr_sem.at[k + shift * pieces], device_id=(g, to * 2 + c),
-            device_id_type=MESH,
-        )
-
-    right = functools.partial(hop, send=rsend, recv=rrecv, s_sem=rs_sem, shift=1)
-    left = functools.partial(hop, send=lsend, recv=lrecv, s_sem=ls_sem, shift=0)
-
-    def pass_on(chip, q, first, to, make, send, recv):
-        k = chip * pieces + q
-        if not first:
-            make(chip, q, to).wait_recv()
-
-        @pl.loop(0, rows // strip)
-        def _(n):
-            at = pl.ds(pl.multiple_of(n * strip, strip), strip)
-            value = own[k, at] + precv[k, at].astype(F32)
-            if not first:
-                value = value + recv[k, at].astype(F32)
-            send[k, at] = value.astype(BF16)
-
-        make(chip, q, to).start()
-
-    sent = set()
+            src_ref=(rsend if to_right else lsend).at[k], dst_ref=landing,
+            send_sem=(rs_sem if to_right else ls_sem).at[0], recv_sem=arrival,
+            device_id=(g, to * 2 + c), device_id_type=MESH,
+        ), landing
+
+    def send(core, a, b, q):
+        if (core, a, b, q) in sent:
+            return
+        sent.add((core, a, b, q))
+        before = a - 1 if b > a else a + 1
+        joins = 0 <= before < chips and not (leaps(core, b) and abs(b - a) == 1)
+
+        @pl.when((c == core) & (z == a))
+        def _():
+            k = b * pieces + q
+            if joins:
+                copy, landed = hop(core, before, b, q)
+                copy.wait_recv()
+            out = rsend if b > a else lsend
+
+            @pl.loop(0, rows // strip)
+            def _(n):
+                at = pl.ds(pl.multiple_of(n * strip, strip), strip)
+                value = own[k, at] + precv[k, at].astype(F32)
+                if joins:
+                    value = value + landed[at].astype(F32)
+                out[k, at] = value.astype(BF16)
+
+            hop(core, a, b, q)[0].start()
 
     def send_first(core, turn, q):
-        if turn >= last_chip or ("first", core, turn, q) in sent:
-            return
-        sent.add(("first", core, turn, q))
-
-        @pl.when((c == core) & (z == 0))
-        def _():
-            pass_on(chips - 1 - turn, q, True, z + 1, right, rsend, rrecv)
-
-        @pl.when((c == core) & (z == last_chip))
-        def _():
-            pass_on(turn, q, True, z - 1, left, lsend, lrecv)
-
-    def send_on(core, turn, q):
-        if turn == 0 or turn >= last_chip or ("on", core, turn, q) in sent:
-            return
-        sent.add(("on", core, turn, q))
-
-        @pl.when((c == core) & low & (z > 0) & (z <= turn))
-        def _():
-            pass_on(chips - 1 - turn + z, q, False, z + 1, right, rsend, rrecv)
-
-        @pl.when((c == core) & high & (z < last_chip) & (last_chip - z <= turn))
-        def _():
-            pass_on(turn - chips + 1 + z, q, False, z - 1, left, lsend, lrecv)
-
-    def send_long(core, turn, q):
-        if turn < chips - chips // 2 or turn >= last_chip or ("long", core, turn, q) in sent:
-            return
-        sent.add(("long", core, turn, q))
-
-        @pl.when((c == core) & high & (z <= turn))
-        def _():
-            pass_on(chips - 1 - turn + z, q, False, z + 1, right, rsend, rrecv)
-
-        @pl.when((c == core) & low & (last_chip - z <= turn))
-        def _():
-            pass_on(turn - chips + 1 + z, q, False, z - 1, left, lsend, lrecv)
-
-    wave = 2 if pieces % 2 == 0 else 1
+        if turn < last_chip:
+            send(core, 0, last_chip - turn, q)
+            send(core, last_chip, turn, q)
+
+    def send_relay(core, d, q):
+        if 0 < d < last_chip:
+            send(core, d, last_chip, q)
+            send(core, last_chip - d, 0, q)
+
+    def send_low(core, q):
+        if chips > 3:
+            send(core, 1, 2, q)
+
+    def send_high(core, q):
+        if chips > 3:
+            send(core, last_chip - 1, last_chip - 2, q)
 
     steps = [(i, q) for i in range(chips) for q in range(0, pieces, wave)]
 
@@ -383,8 +386,7 @@
         @pl.when(c != phase)
         def _():
             product(block, q, psend, k)
-            if phase + n > 0:
-                send_other(n)
+            send_other(n)
 
     def send_other(n):
         i, q = steps[n]
@@ -393,12 +395,17 @@
 
     def settle(phase, n):
         i, first = steps[n]
-        for q in range(first, first + wave):
-            @pl.when(c == phase)
-            def _():
-                pair_copy(block_chip(i), q).wait_recv()
-
-            if phase == 0:
+        both = pl.ds(block_chip(i) * pieces + first, wave)
+
+        @pl.when(c == phase)
+        def _():
+            all_of(
+                psend.at[both], precv.at[both], ps_sem.at[0],
+                pr_sem.at[block_chip(i) * (pieces // wave) + first // wave],
+            ).wait_recv()
+
+        if phase == 0 and i < HELD:
+            for q in range(first, first + wave):
                 send_first(0, i, q)
 
     lane_number = (lax.broadcasted_iota(jnp.int32, (slots, LANES), 1) // rank + 1).astype(F32)
@@ -460,7 +467,7 @@
         @pl.when(c == 1)
         def _():
             term_pair(h).wait_recv()
-            arz[h, z] = packed[h] + arp[h]
+            arz[h, z] = (packed[h] + arp[h]).astype(BF16)
             term_copy(h, 0, 0).start()
             for k in range(1, chips):
                 for core in range(2):
@@ -483,9 +490,9 @@
 
     def expand_rows(h):
         terms_wait(h)
-        total = arz[h, 0]
+        total = arz[h, 0].astype(F32)
         for k in range(1, chips):
-            total = total + arz[h, k]
+            total = total + arz[h, k].astype(F32)
         total = total.astype(BF16).astype(F32)
         if h == 0:
             up_copy.wait()
@@ -514,15 +521,8 @@
         x_copy.wait()
     with scope("place0"):
         place_rows(0)
-    with scope("project0_0"):
-        project(0, 0)
     with scope("enter"):
         enter()
-
-    @pl.when(c == 1)
-    def _():
-        send_other(0)
-
     if rounds:
         tell(0)
     greet_ends()
@@ -550,11 +550,11 @@
         "project": project, "settle": settle, "place": place_rows, "near": near_rows,
         "far": far_rows, "greet": greet_chips, "meet": meet_chips, "factors": load_factors,
         "shrink": shrink_rows, "sum": sum_send, "expand": expand_rows,
-        "first": send_first, "on": send_on, "long": send_long, "requests": requests,
+        "first": send_first, "relay": send_relay, "low": send_low, "high": send_high, "requests": requests,
     }
     for name, *at in ORDER:
-        if name in ("first", "on", "long"):
-            if at[2] >= pieces:
+        if name in ("first", "relay", "low", "high"):
+            if at[-1] >= pieces:
                 continue
         elif name in ("project", "settle"):
             if at[1] >= len(steps):
@@ -563,12 +563,11 @@
             continue
         with scope(name + "_".join(str(v) for v in at)):
             stages[name](*at)
-    for turn in range(last_chip):
-        for q in range(pieces):
+    for b in range(chips):
+        for a in list(range(b)) + list(range(last_chip, b, -1)):
             for core in range(2):
-                send_first(core, turn, q)
-                send_long(core, turn, q)
-                send_on(core, turn, q)
+                for q in range(pieces):
+                    send(core, a, b, q)
 
     res_copy.wait()
 
@@ -580,6 +579,33 @@
         first = q * piece + n * tile
         back = eback[h, :, :, first:first + tile].reshape(slots, tile)
         return jnp.dot(unplace, back, preferred_element_type=F32)
+
+    def close(core, q, into):
+        for a in range(chips):
+            @pl.when((c == core) & (z == a))
+            def _():
+                landed = []
+                for step in (1, 2):
+                    for source in (a - step, a + step):
+                        if 0 <= source < chips and (step == 1 or leaps(core, a)):
+                            copy, ref = hop(core, source, a, q)
+                            copy.wait_recv()
+                            landed.append(ref)
+
+                @pl.loop(0, rows // strip)
+                def _(n):
+                    at = pl.ds(pl.multiple_of(n * strip, strip), strip)
+                    value = own[a * pieces + q, at]
+                    for ref in landed:
+                        value = value + ref[at].astype(F32)
+                    if into is own:
+                        own[a * pieces + q, at] = value
+                    else:
+                        out_ref[at, q * piece:(q + 1) * piece] = value.astype(BF16)
+
+    with scope("close0"):
+        for q in range(pieces):
+            close(0, q, own)
 
     for h in range(halves):
         with scope("backwait%d" % h):
@@ -595,42 +621,12 @@
                         + rbuf[:, first:first + tile].astype(F32)
                     )
                 own[z * pieces + q, :, cols] = value
+                if h == halves - 1:
+                    out_ref[:, first:first + tile] = value.astype(BF16)
 
     for q in range(pieces):
-        mine_at = z * pieces + q
-        mark = scope("fin%d" % q)
-        mark.__enter__()
-
-        def finish(use_right, use_left):
-            @pl.loop(0, rows // strip)
-            def _(n):
-                at = pl.ds(pl.multiple_of(n * strip, strip), strip)
-                value = own[mine_at, at]
-                if use_right:
-                    value = value + rrecv[mine_at, at].astype(F32)
-                if use_left:
-                    value = value + lrecv[mine_at, at].astype(F32)
-                out_ref[at, q * piece:(q + 1) * piece] = value.astype(BF16)
-
-        if chips == 1:
-            finish(False, False)
-        else:
-            @pl.when(z == 0)
-            def _():
-                left(z, q, z).wait_recv()
-                finish(False, True)
-
-            @pl.when(z == chips - 1)
-            def _():
-                right(z, q, z).wait_recv()
-                finish(True, False)
-
-            @pl.when((z > 0) & (z < chips - 1))
-            def _():
-                right(z, q, z).wait_recv()
-                left(z, q, z).wait_recv()
-                finish(True, True)
-        mark.__exit__(None, None, None)
+        with scope("fin%d" % q):
+            close(1, q, out_ref)
 
     tail = scope("tail")
     tail.__enter__()
@@ -712,16 +708,18 @@
             pltpu.VMEM((hops, rows, piece), BF16),
             pltpu.VMEM((hops, rows, piece), BF16),
             pltpu.VMEM((hops, rows, piece), BF16),
+            pltpu.VMEM((pieces, rows, piece), BF16),
+            pltpu.VMEM((pieces, rows, piece), BF16),
             pltpu.VMEM((halves, groups, part, depth), BF16),
             pltpu.VMEM((halves, groups, part, depth), BF16),
             pltpu.VMEM((halves, slots, LANES), F32),
             pltpu.VMEM((halves, rank, slots), F32),
             pltpu.VMEM((halves, rank, slots), F32),
-            pltpu.VMEM((halves, chips, rank, slots), F32),
+            pltpu.VMEM((halves, chips, rank, slots), BF16),
             pltpu.VMEM((halves, groups, part, width), BF16),
             pltpu.VMEM((halves, groups, part, width), BF16),
-            dma((AHEAD,)), dma((3,)), dma((1,)), dma((hops,)),
-            dma((1,)), dma((1,)), dma((hops + pieces,)),
+            dma((AHEAD,)), dma((3,)), dma((1,)), dma((hops // (2 if pieces % 2 == 0 else 1),)),
+            dma((1,)), dma((1,)), dma((hops + pieces,)), dma((2 * pieces,)),
             dma((1,)), dma((halves,)), dma((1,)), dma((halves,)),
             dma((1,)), dma((halves,)), dma((1,)), dma((halves,)),
             pltpu.SemaphoreType.REGULAR((max(1, groups.bit_length() - 2),)),

time: 27.5 us -> 26.3 us (0.956)
  the two profiles are of different devices: /device:TPU:1 before, /device:TPU:0 now
where the time goes in v3:
time: 26.3 us; the launch traced here: 26.1 us
  Pallas kernels  25.4 us (97%)
  local copies, waits for them, and re-layouts  0.71 us (3%)
    pallas_call x1, Pallas kernels, body(): pl.pallas_call(functools.partial(kernel, groups, members, rank, owned, ha...  25.4 us
    unnamed x1, local copies, waits for them, and re-layouts  0.71 us

profile of v3, /device:TPU:0, one launch (start us, length us, event | category | flops | bytes accessed | tf_op | source)
XLA Modules:
  0.0 26.1 jit_solution(3952045096854658429)
XLA Ops:
  0.0 25.4 %shard_map.64 = bf16[128,1024]{1,0:T(8,128)(2,1)S(1)} custom-call(bf16[128,1024]{1,0:T(8,128)(2,1)} %x_hbm.1, bf16[128,1024]{1,0:T(8,128)(2,1)} %res_ref.1, s32[1,128]{1,0:T(1,128)} %bitcast.7, bf16[1024,8192]{1,0:T(8,128)(2,1)} %w_ref.1, bf16[1024,1024]{1,0:T(8,128)(2,1)} %bitcast.5, bf16[1024,1024]{1,0:T(8,128)(2,1)} %bitcast.6), custom_call_target="tpu_custom_call" | custom-call | tf_op jit(solution)/shard_map/pallas_call | solution.py:691
  25.4 0.7 %copy.8 = bf16[128,1024]{1,0:T(8,128)(2,1)} copy(bf16[128,1024]{1,0:T(8,128)(2,1)S(1)} %shard_map.64) | data formatting | bytes 524288

commit v4 on v3

--- a/solution.py
+++ b/solution.py
@@ -19,31 +19,23 @@
 ORDER = (
     ("near", 0), ("project", 0, 0), ("project", 0, 1), ("project", 0, 2), ("settle", 0, 0),
     ("far", 0), ("project", 0, 3), ("settle", 0, 1), ("place", 1), ("factors",),
-    ("project", 0, 4), ("settle", 0, 2), ("project", 0, 5), ("settle", 0, 3),
-    ("far", 1), ("near", 1),
-    ("project", 1, 0), ("project", 0, 6), ("settle", 0, 4), ("greet",), ("project", 0, 7),
-    ("settle", 0, 5), ("settle", 0, 6), ("settle", 0, 7),
-    ("relay", 0, 2, 0), ("relay", 0, 2, 1), ("relay", 0, 2, 2), ("relay", 0, 2, 3),
-    ("requests",), ("relay", 0, 1, 0), ("relay", 0, 1, 1),
-    ("shrink", 0), ("settle", 1, 0), ("first", 1, 0, 0), ("first", 0, 2, 0), ("first", 0, 2, 1),
-    ("relay", 0, 1, 2), ("relay", 0, 1, 3),
-    ("project", 1, 1), ("low", 0, 0), ("low", 0, 1), ("project", 1, 2),
-    ("meet",), ("sum", 0), ("project", 1, 3),
-    ("first", 1, 0, 1), ("settle", 1, 1), ("first", 1, 0, 2),
-    ("shrink", 1), ("project", 1, 4), ("sum", 1),
-    ("low", 0, 2), ("low", 0, 3), ("first", 1, 0, 3), ("project", 1, 5),
-    ("relay", 1, 1, 0), ("project", 1, 6), ("project", 1, 7),
-    ("settle", 1, 2), ("settle", 1, 3),
-    ("first", 1, 1, 0), ("first", 1, 1, 1), ("first", 1, 1, 2), ("first", 1, 1, 3),
-    ("settle", 1, 4), ("settle", 1, 5),
+    ("project", 0, 4), ("settle", 0, 2), ("project", 0, 5), ("settle", 0, 3), ("far", 1),
+    ("near", 1), ("project", 1, 0), ("project", 0, 6), ("settle", 0, 4), ("greet",),
+    ("project", 0, 7), ("settle", 0, 5), ("settle", 0, 6), ("settle", 0, 7), ("relay", 0, 2, 0),
+    ("relay", 0, 2, 1), ("relay", 0, 2, 2), ("relay", 0, 2, 3), ("requests",), ("relay", 0, 1, 0),
+    ("relay", 0, 1, 1), ("shrink", 0), ("settle", 1, 0), ("first", 1, 0, 0), ("first", 0, 2, 0),
+    ("first", 0, 2, 1), ("relay", 0, 1, 2), ("relay", 0, 1, 3), ("project", 1, 1), ("low", 0, 0),
+    ("low", 0, 1), ("project", 1, 2), ("meet",), ("sum", 0), ("project", 1, 3), ("settle", 1, 1),
+    ("first", 1, 0, 1), ("first", 1, 0, 2), ("shrink", 1), ("project", 1, 4), ("high", 0, 0),
+    ("high", 0, 1), ("sum", 1), ("low", 0, 2), ("low", 0, 3), ("first", 1, 0, 3),
+    ("settle", 1, 2), ("first", 1, 1, 0), ("first", 1, 1, 1), ("settle", 1, 3), ("project", 1, 5),
+    ("relay", 1, 1, 0), ("project", 1, 6), ("project", 1, 7), ("high", 0, 2), ("high", 0, 3),
+    ("first", 1, 1, 2), ("first", 1, 1, 3), ("settle", 1, 4), ("settle", 1, 5),
     ("first", 1, 2, 0), ("first", 1, 2, 1), ("first", 1, 2, 2), ("first", 1, 2, 3),
-    ("settle", 1, 6), ("settle", 1, 7),
-    ("expand", 0), ("high", 0, 0), ("high", 0, 1), ("high", 0, 2), ("high", 0, 3),
-    ("relay", 1, 1, 1), ("relay", 1, 1, 2),
-    ("relay", 1, 2, 0), ("relay", 1, 2, 1), ("relay", 1, 2, 2), ("relay", 1, 2, 3),
-    ("expand", 1), ("relay", 1, 1, 3), ("first", 0, 2, 2), ("first", 0, 2, 3),
-    ("low", 1, 0), ("high", 1, 0), ("low", 1, 1), ("high", 1, 1),
-    ("low", 1, 2), ("high", 1, 2), ("low", 1, 3), ("high", 1, 3),
+    ("settle", 1, 6), ("settle", 1, 7), ("expand", 0), ("relay", 1, 1, 1), ("relay", 1, 1, 2),
+    ("relay", 1, 2, 0), ("relay", 1, 2, 1), ("relay", 1, 2, 2), ("relay", 1, 2, 3), ("expand", 1),
+    ("relay", 1, 1, 3), ("first", 0, 2, 2), ("first", 0, 2, 3), ("low", 1, 0), ("high", 1, 0),
+    ("low", 1, 1), ("high", 1, 1), ("low", 1, 2), ("high", 1, 2), ("low", 1, 3), ("high", 1, 3),
 )
 scope = contextlib.nullcontext
 
@@ -374,6 +366,12 @@
             ).astype(into.dtype)
 
     def project(phase, n):
+        if phase + n == 0:
+            @pl.when(c == 0)
+            def _():
+                product(0, 0, own, first_at)
+
+            return
         i, q = steps[n]
         block = phase * chips + i
         k = block_chip(i) * pieces + q
@@ -473,10 +471,10 @@
                 for core in range(2):
                     term_copy(h, k, core).start()
 
-    def back_copy(h, k):
+    def back_copy(h, k, cols):
         to = peer(k)
         return pltpu.make_async_remote_copy(
-            src_ref=esend.at[h, to], dst_ref=eback.at[h, g],
+            src_ref=esend.at[h, to, :, cols], dst_ref=eback.at[h, g, :, cols],
             send_sem=es_sem.at[0], recv_sem=er_sem.at[h],
             device_id=(to, t), device_id_type=MESH,
         )
@@ -506,23 +504,35 @@
             axis=1,
         )
 
-        @pl.loop(0, width // wide)
-        def _(n):
-            cols = pl.ds(pl.multiple_of(n * wide, LANES), wide)
-            grown = jnp.dot(spread, ubuf[:, cols], preferred_element_type=F32).astype(BF16)
+        for n in range(width // wide):
+            cols = pl.ds(n * wide, wide)
+            grown = jnp.dot(
+                spread, ubuf[:, n * wide:(n + 1) * wide], preferred_element_type=F32
+            ).astype(BF16)
             for k in range(groups):
                 esend[h, k, :, cols] = grown[k * part:(k + 1) * part]
-
-        for k in far + near:
-            back_copy(h, k).start()
+            for k in far + near:
+                back_copy(h, k, cols).start()
         eback[h, g] = esend[h, g]
 
     with scope("x"):
         x_copy.wait()
+    first_at = block_chip(0) * pieces
+    weights(0, 0)
+
+    @pl.when(c == 1)
+    def _():
+        product(0, 0, psend, first_at)
+
+    with scope("enter"):
+        enter()
+
+    @pl.when(c == 1)
+    def _():
+        send_other(0)
+
     with scope("place0"):
         place_rows(0)
-    with scope("enter"):
-        enter()
     if rounds:
         tell(0)
     greet_ends()

time: 26.3 us -> 26.2 us (level)
  no operation moved by 1% of the time
where the time goes in v4:
time: 26.2 us; the launch traced here: 26.1 us
  Pallas kernels  25.4 us (97%)
  local copies, waits for them, and re-layouts  0.71 us (3%)
    pallas_call x1, Pallas kernels, body(): pl.pallas_call(functools.partial(kernel, groups, members, rank, owned, ha...  25.4 us
    unnamed x1, local copies, waits for them, and re-layouts  0.71 us

profile of v4, /device:TPU:0, one launch (start us, length us, event | category | flops | bytes accessed | tf_op | source)
XLA Modules:
  0.0 26.1 jit_solution(5744598994163415700)
XLA Ops:
  0.0 25.4 %shard_map.64 = bf16[128,1024]{1,0:T(8,128)(2,1)S(1)} custom-call(bf16[128,1024]{1,0:T(8,128)(2,1)} %x_hbm.1, bf16[128,1024]{1,0:T(8,128)(2,1)} %res_ref.1, s32[1,128]{1,0:T(1,128)} %bitcast.7, bf16[1024,8192]{1,0:T(8,128)(2,1)} %w_ref.1, bf16[1024,1024]{1,0:T(8,128)(2,1)} %bitcast.5, bf16[1024,1024]{1,0:T(8,128)(2,1)} %bitcast.6), custom_call_target="tpu_custom_call" | custom-call | tf_op jit(solution)/shard_map/pallas_call | solution.py:701
  25.4 0.7 %copy.8 = bf16[128,1024]{1,0:T(8,128)(2,1)} copy(bf16[128,1024]{1,0:T(8,128)(2,1)S(1)} %shard_map.64) | data formatting | bytes 524288

commit v5 on v4

--- a/solution.py
+++ b/solution.py
@@ -43,7 +43,7 @@
 def kernel(
     groups, members, rank, owned, halves, pieces,
     x_hbm, res_ref, idx_hbm, w_ref, down_ref, up_ref, out_ref,
-    x_ref, idx_ref, idx_all, wbuf, dbuf, ubuf, rbuf, own, psend, precv, rrecv, lrecv, rsend, lsend, jrecv, klrecv,
+    x_ref, idx_ref, idx_all, wbuf, dbuf, ubuf, rbuf, own, psend, precv, rrecv, lrecv, rsend, lsend, jrecv,
     xsend, xrecv, wants, packed, arp, arz, esend, eback,
     w_sem, d_sem, ps_sem, pr_sem, rs_sem, ls_sem, hr_sem, j_sem,
     xs_sem, xr_sem, as_sem, ar_sem, zs_sem, zr_sem, es_sem, er_sem, dp_sem, z_sem, is_sem, ir_sem,
@@ -302,8 +302,8 @@
         jump = leaps(core, b) and abs(b - a) == 2
         to = b if jump else (a + 1 if to_right else a - 1)
         if jump:
-            landing = (jrecv if to_right else klrecv).at[q]
-            arrival = j_sem.at[q + (0 if to_right else pieces)]
+            landing = jrecv.at[q]
+            arrival = j_sem.at[q]
         else:
             landing = (rrecv if to_right else lrecv).at[k]
             arrival = hr_sem.at[k + (pieces if to_right else 0)]
@@ -719,7 +719,6 @@
             pltpu.VMEM((hops, rows, piece), BF16),
             pltpu.VMEM((hops, rows, piece), BF16),
             pltpu.VMEM((pieces, rows, piece), BF16),
-            pltpu.VMEM((pieces, rows, piece), BF16),
             pltpu.VMEM((halves, groups, part, depth), BF16),
             pltpu.VMEM((halves, groups, part, depth), BF16),
             pltpu.VMEM((halves, slots, LANES), F32),
@@ -729,7 +728,7 @@
             pltpu.VMEM((halves, groups, part, width), BF16),
             pltpu.VMEM((halves, groups, part, width), BF16),
             dma((AHEAD,)), dma((3,)), dma((1,)), dma((hops // (2 if pieces % 2 == 0 else 1),)),
-            dma((1,)), dma((1,)), dma((hops + pieces,)), dma((2 * pieces,)),
+            dma((1,)), dma((1,)), dma((hops + pieces,)), dma((pieces,)),
             dma((1,)), dma((halves,)), dma((1,)), dma((halves,)),
             dma((1,)), dma((halves,)), dma((1,)), dma((halves,)),
             pltpu.SemaphoreType.REGULAR((max(1, groups.bit_length() - 2),)),

time: 26.2 us -> 26.2 us (level)
  no operation moved by 1% of the time
where the time goes in v5:
time: 26.2 us; the launch traced here: 26 us
  Pallas kernels  25.3 us (97%)
  local copies, waits for them, and re-layouts  0.71 us (3%)
    pallas_call x1, Pallas kernels, body(): pl.pallas_call(functools.partial(kernel, groups, members, rank, owned, ha...  25.3 us
    unnamed x1, local copies, waits for them, and re-layouts  0.71 us

profile of v5, /device:TPU:0, one launch (start us, length us, event | category | flops | bytes accessed | tf_op | source)
XLA Modules:
  0.0 26.0 jit_solution(10004832458160032652)
XLA Ops:
  0.0 25.3 %shard_map.64 = bf16[128,1024]{1,0:T(8,128)(2,1)S(1)} custom-call(bf16[128,1024]{1,0:T(8,128)(2,1)} %x_hbm.1, bf16[128,1024]{1,0:T(8,128)(2,1)} %res_ref.1, s32[1,128]{1,0:T(1,128)} %bitcast.7, bf16[1024,8192]{1,0:T(8,128)(2,1)} %w_ref.1, bf16[1024,1024]{1,0:T(8,128)(2,1)} %bitcast.5, bf16[1024,1024]{1,0:T(8,128)(2,1)} %bitcast.6), custom_call_target="tpu_custom_call" | custom-call | tf_op jit(solution)/shard_map/pallas_call | solution.py:701
  25.3 0.7 %copy.8 = bf16[128,1024]{1,0:T(8,128)(2,1)} copy(bf16[128,1024]{1,0:T(8,128)(2,1)S(1)} %shard_map.64) | data formatting | bytes 524288

commit v6 on v5

--- a/solution.py
+++ b/solution.py
@@ -26,8 +26,8 @@
     ("relay", 0, 1, 1), ("shrink", 0), ("settle", 1, 0), ("first", 1, 0, 0), ("first", 0, 2, 0),
     ("first", 0, 2, 1), ("relay", 0, 1, 2), ("relay", 0, 1, 3), ("project", 1, 1), ("low", 0, 0),
     ("low", 0, 1), ("project", 1, 2), ("meet",), ("sum", 0), ("project", 1, 3), ("settle", 1, 1),
-    ("first", 1, 0, 1), ("first", 1, 0, 2), ("shrink", 1), ("project", 1, 4), ("high", 0, 0),
-    ("high", 0, 1), ("sum", 1), ("low", 0, 2), ("low", 0, 3), ("first", 1, 0, 3),
+    ("first", 1, 0, 1), ("shrink", 1), ("project", 1, 4), ("high", 0, 0), ("high", 0, 1),
+    ("sum", 1), ("first", 1, 0, 2), ("low", 0, 2), ("low", 0, 3), ("first", 1, 0, 3),
     ("settle", 1, 2), ("first", 1, 1, 0), ("first", 1, 1, 1), ("settle", 1, 3), ("project", 1, 5),
     ("relay", 1, 1, 0), ("project", 1, 6), ("project", 1, 7), ("high", 0, 2), ("high", 0, 3),
     ("first", 1, 1, 2), ("first", 1, 1, 3), ("settle", 1, 4), ("settle", 1, 5),
@@ -466,10 +466,10 @@
         def _():
             term_pair(h).wait_recv()
             arz[h, z] = (packed[h] + arp[h]).astype(BF16)
+            for core in range(2):
+                for k in range(1, chips):
+                    term_copy(h, k, core).start()
             term_copy(h, 0, 0).start()
-            for k in range(1, chips):
-                for core in range(2):
-                    term_copy(h, k, core).start()
 
     def back_copy(h, k, cols):
         to = peer(k)

time: 26.2 us -> 25.6 us (0.977)
  Pallas kernels: 25.3 us -> 24.7 us
    pallas_call x1, Pallas kernels: 25.3 us -> 24.7 us  [body(): pl.pallas_call(functools.partial(kernel, groups, members, rank, owned, ha...]
where the time goes in v6:
time: 25.6 us; the launch traced here: 25.5 us
  Pallas kernels  24.7 us (96%)
  local copies, waits for them, and re-layouts  0.71 us (3%)
    pallas_call x1, Pallas kernels, body(): pl.pallas_call(functools.partial(kernel, groups, members, rank, owned, ha...  24.7 us
    unnamed x1, local copies, waits for them, and re-layouts  0.71 us

profile of v6, /device:TPU:0, one launch (start us, length us, event | category | flops | bytes accessed | tf_op | source)
XLA Modules:
  0.0 25.5 jit_solution(1093417857582626811)
XLA Ops:
  0.0 24.7 %shard_map.64 = bf16[128,1024]{1,0:T(8,128)(2,1)S(1)} custom-call(bf16[128,1024]{1,0:T(8,128)(2,1)} %x_hbm.1, bf16[128,1024]{1,0:T(8,128)(2,1)} %res_ref.1, s32[1,128]{1,0:T(1,128)} %bitcast.7, bf16[1024,8192]{1,0:T(8,128)(2,1)} %w_ref.1, bf16[1024,1024]{1,0:T(8,128)(2,1)} %bitcast.5, bf16[1024,1024]{1,0:T(8,128)(2,1)} %bitcast.6), custom_call_target="tpu_custom_call" | custom-call | tf_op jit(solution)/shard_map/pallas_call | solution.py:701
  24.7 0.7 %copy.8 = bf16[128,1024]{1,0:T(8,128)(2,1)} copy(bf16[128,1024]{1,0:T(8,128)(2,1)S(1)} %shard_map.64) | data formatting | bytes 524288

commit v7 on v6

--- a/solution.py
+++ b/solution.py
@@ -25,17 +25,18 @@
     ("relay", 0, 2, 1), ("relay", 0, 2, 2), ("relay", 0, 2, 3), ("requests",), ("relay", 0, 1, 0),
     ("relay", 0, 1, 1), ("shrink", 0), ("settle", 1, 0), ("first", 1, 0, 0), ("first", 0, 2, 0),
     ("first", 0, 2, 1), ("relay", 0, 1, 2), ("relay", 0, 1, 3), ("project", 1, 1), ("low", 0, 0),
-    ("low", 0, 1), ("project", 1, 2), ("meet",), ("sum", 0), ("project", 1, 3), ("settle", 1, 1),
-    ("first", 1, 0, 1), ("shrink", 1), ("project", 1, 4), ("high", 0, 0), ("high", 0, 1),
-    ("sum", 1), ("first", 1, 0, 2), ("low", 0, 2), ("low", 0, 3), ("first", 1, 0, 3),
-    ("settle", 1, 2), ("first", 1, 1, 0), ("first", 1, 1, 1), ("settle", 1, 3), ("project", 1, 5),
-    ("relay", 1, 1, 0), ("project", 1, 6), ("project", 1, 7), ("high", 0, 2), ("high", 0, 3),
-    ("first", 1, 1, 2), ("first", 1, 1, 3), ("settle", 1, 4), ("settle", 1, 5),
-    ("first", 1, 2, 0), ("first", 1, 2, 1), ("first", 1, 2, 2), ("first", 1, 2, 3),
-    ("settle", 1, 6), ("settle", 1, 7), ("expand", 0), ("relay", 1, 1, 1), ("relay", 1, 1, 2),
-    ("relay", 1, 2, 0), ("relay", 1, 2, 1), ("relay", 1, 2, 2), ("relay", 1, 2, 3), ("expand", 1),
-    ("relay", 1, 1, 3), ("first", 0, 2, 2), ("first", 0, 2, 3), ("low", 1, 0), ("high", 1, 0),
-    ("low", 1, 1), ("high", 1, 1), ("low", 1, 2), ("high", 1, 2), ("low", 1, 3), ("high", 1, 3),
+    ("low", 0, 1), ("project", 1, 2), ("meet",), ("sum", 0), ("first", 1, 0, 1),
+    ("project", 1, 3), ("settle", 1, 1), ("shrink", 1), ("project", 1, 4), ("high", 0, 0),
+    ("high", 0, 1), ("sum", 1), ("first", 1, 0, 2), ("low", 0, 2), ("low", 0, 3),
+    ("first", 1, 0, 3), ("settle", 1, 2), ("first", 1, 1, 0), ("first", 1, 1, 1),
+    ("settle", 1, 3), ("project", 1, 5), ("relay", 1, 1, 0), ("project", 1, 6), ("project", 1, 7),
+    ("high", 0, 2), ("high", 0, 3), ("first", 1, 1, 2), ("first", 1, 1, 3), ("settle", 1, 4),
+    ("settle", 1, 5), ("first", 1, 2, 0), ("first", 1, 2, 1), ("first", 1, 2, 2),
+    ("first", 1, 2, 3), ("settle", 1, 6), ("settle", 1, 7), ("expand", 0), ("relay", 1, 1, 1),
+    ("relay", 1, 1, 2), ("relay", 1, 2, 0), ("relay", 1, 2, 1), ("relay", 1, 2, 2),
+    ("relay", 1, 2, 3), ("expand", 1), ("relay", 1, 1, 3), ("first", 0, 2, 2), ("first", 0, 2, 3),
+    ("low", 1, 0), ("high", 1, 0), ("low", 1, 1), ("high", 1, 1), ("low", 1, 2), ("high", 1, 2),
+    ("low", 1, 3), ("high", 1, 3),
 )
 scope = contextlib.nullcontext
 

time: 25.6 us -> 25.6 us (level)
  no operation moved by 1% of the time
where the time goes in v7:
time: 25.6 us; the launch traced here: 25.5 us
  Pallas kernels  24.7 us (96%)
  local copies, waits for them, and re-layouts  0.71 us (3%)
    pallas_call x1, Pallas kernels, body(): pl.pallas_call(functools.partial(kernel, groups, members, rank, owned, ha...  24.7 us
    unnamed x1, local copies, waits for them, and re-layouts  0.71 us

profile of v7, /device:TPU:0, one launch (start us, length us, event | category | flops | bytes accessed | tf_op | source)
XLA Modules:
  0.0 25.5 jit_solution(133852001005639618)
XLA Ops:
  0.0 24.7 %shard_map.64 = bf16[128,1024]{1,0:T(8,128)(2,1)S(1)} custom-call(bf16[128,1024]{1,0:T(8,128)(2,1)} %x_hbm.1, bf16[128,1024]{1,0:T(8,128)(2,1)} %res_ref.1, s32[1,128]{1,0:T(1,128)} %bitcast.7, bf16[1024,8192]{1,0:T(8,128)(2,1)} %w_ref.1, bf16[1024,1024]{1,0:T(8,128)(2,1)} %bitcast.5, bf16[1024,1024]{1,0:T(8,128)(2,1)} %bitcast.6), custom_call_target="tpu_custom_call" | custom-call | tf_op jit(solution)/shard_map/pallas_call | solution.py:702
  24.7 0.7 %copy.8 = bf16[128,1024]{1,0:T(8,128)(2,1)} copy(bf16[128,1024]{1,0:T(8,128)(2,1)S(1)} %shard_map.64) | data formatting | bytes 524288
